TPU v7x, 32 devices: a whole 2x2x4 slice. The times are simulated.
32 devices in a mesh: expert: 4 (over z), tensor: 4 (over y, x), dp: 2 (over core).
Axes of the slice: x: 2, y: 2, z: 4, core: 2. Of those that a mesh axis runs over, the one named last changes fastest.
Arguments:
- hidden_in: bfloat16 [2, 512, 4096], P('dp', 'expert'), may hold values from -64 to 64
- expert_ids: int32 [2, 512, 2], P('dp', 'expert'), may hold values from 0 to 3, all different within a row; in each aligned block of 128 rows (0 to 127, 128 to 255, ..., all dimensions but the last counted through in order) at most 72 rows name the same one
- ffn_gain: float32 [4096], replicated, may hold values from 0.5 to 1.5
- w_router: bfloat16 [4096, 4], replicated, may hold values from -0.09375 to 0.09375
- w_gate: bfloat16 [4, 4096, 14336], P('expert', None, ('tensor', 'dp')), may hold values from -0.09375 to 0.09375
- w_up: bfloat16 [4, 4096, 14336], P('expert', None, ('tensor', 'dp')), may hold values from -0.09375 to 0.09375
- w_down: bfloat16 [4, 14336, 4096], P('expert', ('tensor', 'dp')), may hold values from -0.046875 to 0.046875
Outputs:
- hidden_out: bfloat16 [2, 512, 4096], P('dp', 'expert', 'tensor')
- layer_score: float32 [], replicated
Inputs may be any that keep to these rules, and one draw needn't show every extreme that they name: `expert_ids`: among the 128 tokens of one device (aligned blocks of the flattened sequence and position order), no expert is chosen by more than 72 of them; a token's two experts differ.
All inputs are finite; a program needn't handle non-finite values.
Results may differ from a plain program's by a relative error of at most 0.0027.
Values may be sent and summed in bfloat16 or wider, within the bound.
No kernel may reach another device: no remote copies, remote signals or barrier semaphores. Data moves between devices by JAX's collectives and lax.ppermute only.
A program may use at most 128 MiB of HBM per device.

v0:
```python
import functools
import jax
import jax.numpy as jnp
from jax import lax
from jax.experimental import pallas as pl
from jax.experimental.pallas import tpu as pltpu
from jax.sharding import PartitionSpec as P

EPS_NORM = 1e-05
EPS_COS = 1e-06
AHEAD = 2


def slot_positions(flat_ids, experts):
    pair_count = flat_ids.shape[0]
    onehot = (flat_ids[:, None] == jnp.arange(experts, dtype=jnp.int32)[None, :]).astype(jnp.int32)
    positions = jnp.arange(pair_count, dtype=jnp.int32)
    earlier = (positions[None, :] < positions[:, None]).astype(jnp.int32)
    before = jnp.sum(earlier[:, :, None] * onehot[None, :, :], axis=1)
    return jnp.sum(before * onehot, axis=1)


def swap(value, axis, step):
    count = lax.axis_size(axis)
    return lax.ppermute(value, axis, [(i, i ^ step) for i in range(count)])


def tile_of(size, most):
    for tile in range(most, 127, -128):
        if size % tile == 0:
            return tile
    return size


def expert_kernel(groups, parts, shares, f_tiles, n_tiles, t_ref, *refs):
    sources = refs[:groups]
    w_gate, w_up, w_down = refs[groups : groups + 3]
    results = refs[groups + 3 : groups + 3 + groups * len(parts)]
    (rows_ref, act_ref, out_ref, gate_buf, up_buf, down_buf) = refs[-10:-4]
    row_sems, in_sems, down_sems, out_sems = refs[-4:]
    rows = sources[0].shape[0]
    share = sources[0].shape[1] // shares
    f_tile = gate_buf.shape[2]
    n_tile = down_buf.shape[2]
    per = share // n_tile

    def row_copy(d, j):
        at = pl.multiple_of(jnp.bitwise_xor(t_ref[0], j) * share, share)
        return pltpu.make_async_copy(
            sources[d].at[:, pl.ds(j * share, share)],
            rows_ref.at[pl.ds(d * rows, rows), pl.ds(at, share)],
            row_sems.at[d, j],
        )

    def in_copy(weight, buffer, which, f):
        source = weight
        if f_tiles > 1:
            source = weight.at[:, pl.ds(pl.multiple_of(f * f_tile, f_tile), f_tile)]
        slot = lax.rem(f, gate_buf.shape[0])
        return pltpu.make_async_copy(source, buffer.at[slot], in_sems.at[which, slot])

    def down_copy(n):
        at = (jnp.bitwise_xor(t_ref[0], n // per) * per + n % per) * n_tile
        slot = lax.rem(n, down_buf.shape[0])
        return pltpu.make_async_copy(
            w_down.at[:, pl.ds(pl.multiple_of(at, n_tile), n_tile)],
            down_buf.at[slot],
            down_sems.at[slot],
        )

    def out_copies(n):
        at = pl.ds(pl.multiple_of(n * n_tile, n_tile), n_tile)
        begin = 0
        copies = []
        for which in range(groups * len(parts)):
            size = parts[which % len(parts)]
            copies.append(
                pltpu.make_async_copy(
                    out_ref.at[n, pl.ds(begin, size)],
                    results[which].at[:, at],
                    out_sems.at[which, n],
                )
            )
            begin += size
        return copies

    def start_hidden(f):
        in_copy(w_gate, gate_buf, 0, f).start()
        in_copy(w_up, up_buf, 1, f).start()

    def start_down(n):
        if isinstance(n, int):
            if n < n_tiles:
                down_copy(n).start()
        else:
            pl.when(n < n_tiles)(lambda: down_copy(n).start())

    for d in range(groups):
        for j in range(shares):
            row_copy(d, j).start()
    start_hidden(0)
    for d in range(groups):
        for j in range(shares):
            row_copy(d, j).wait()
    for f in range(1, min(AHEAD, f_tiles)):
        start_hidden(f)
    for e in range(AHEAD - f_tiles):
        start_down(2 * e)
        start_down(2 * e + 1)

    def hidden_step(f, carry):
        in_copy(w_gate, gate_buf, 0, f).wait()
        in_copy(w_up, up_buf, 1, f).wait()

        @pl.when(f + AHEAD < f_tiles)
        def _():
            start_hidden(f + AHEAD)

        @pl.when(f + AHEAD >= f_tiles)
        def _():
            start_down(2 * (f + AHEAD - f_tiles))
            start_down(2 * (f + AHEAD - f_tiles) + 1)

        slot = lax.rem(f, gate_buf.shape[0])
        gate = jnp.dot(rows_ref[...], gate_buf[slot], preferred_element_type=jnp.float32)
        up = jnp.dot(rows_ref[...], up_buf[slot], preferred_element_type=jnp.float32)
        act = (gate / (1.0 + jnp.exp(-gate)) * up).astype(jnp.bfloat16)
        if f_tiles == 1:
            act_ref[...] = act
        else:
            act_ref[:, pl.ds(pl.multiple_of(f * f_tile, f_tile), f_tile)] = act
        return carry

    def down_step(n, carry):
        down_copy(n).wait()
        start_down(n + 2 * AHEAD)
        out_ref[n] = jnp.dot(act_ref[...], down_buf[lax.rem(n, down_buf.shape[0])], preferred_element_type=jnp.float32)
        for copy in out_copies(n):
            copy.start()
        return carry

    lax.fori_loop(0, f_tiles, hidden_step, 0)
    lax.fori_loop(0, n_tiles, down_step, 0)
    for n in range(n_tiles):
        for copy in out_copies(n):
            copy.wait()


def run_expert(sources, w_gate, w_up, w_down, tensor_index, shares, parts):
    groups = len(sources)
    rows, width = sources[0].shape
    hidden = w_gate.shape[1]
    share = width // shares
    f_tile = tile_of(hidden, 256)
    n_tile = tile_of(share, 512)
    f_tiles, n_tiles = hidden // f_tile, width // n_tile
    total = groups * rows
    in_slots = min(f_tiles, AHEAD + 1)
    down_slots = min(n_tiles, 2 * AHEAD + 1)
    return pl.pallas_call(
        functools.partial(expert_kernel, groups, parts, shares, f_tiles, n_tiles),
        out_shape=[jax.ShapeDtypeStruct((size, width), jnp.float32) for size in parts] * groups,
        in_specs=[pl.BlockSpec(memory_space=pltpu.SMEM)]
        + [pl.BlockSpec(memory_space=pl.ANY)] * (groups + 3),
        out_specs=[pl.BlockSpec(memory_space=pl.ANY)] * (groups * len(parts)),
        scratch_shapes=[
            pltpu.VMEM((total, width), jnp.bfloat16),
            pltpu.VMEM((total, hidden), jnp.bfloat16),
            pltpu.VMEM((n_tiles, total, n_tile), jnp.float32),
            pltpu.VMEM((in_slots, width, f_tile), jnp.bfloat16),
            pltpu.VMEM((in_slots, width, f_tile), jnp.bfloat16),
            pltpu.VMEM((down_slots, hidden, n_tile), jnp.bfloat16),
            pltpu.SemaphoreType.DMA((groups, shares)),
            pltpu.SemaphoreType.DMA((2, in_slots)),
            pltpu.SemaphoreType.DMA((down_slots,)),
            pltpu.SemaphoreType.DMA((groups * len(parts), n_tiles)),
        ],
        compiler_params=pltpu.CompilerParams(vmem_limit_bytes=38 << 20),
        cost_estimate=pl.CostEstimate(
            flops=6 * total * width * hidden,
            bytes_accessed=6 * width * hidden + 6 * total * width,
            transcendentals=total * hidden,
        ),
        name="expert",
    )(tensor_index, *sources, w_gate, w_up, w_down)


def sum_over(value, axis):
    step = 1
    while step < lax.axis_size(axis):
        value = value + swap(value, axis, step)
        step *= 2
    return value


def shards(hidden_in, expert_ids, ffn_gain, w_router, w_gate, w_up, w_down):
    tok_count = hidden_in.shape[1]
    model_width = hidden_in.shape[2]
    top_count = expert_ids.shape[2]
    expert_count = lax.axis_size("expert")
    tensor_count = lax.axis_size("tensor")
    replica_count = lax.axis_size("dp")
    experts = expert_count * w_gate.shape[0]
    capacity = max(2, 9 * tok_count * top_count // (8 * experts))
    share = model_width // tensor_count
    z = lax.axis_index("expert")
    t = lax.axis_index("tensor")
    token_rows = hidden_in.reshape(tok_count, model_width).astype(jnp.float32)
    in_squares = jnp.mean(token_rows * token_rows, axis=1)
    inverse_rms = lax.rsqrt(in_squares[:, None] + EPS_NORM)
    normed = (token_rows * inverse_rms * ffn_gain[None, :]).astype(jnp.bfloat16)
    chosen = expert_ids.reshape(tok_count, top_count)
    slot_index = slot_positions(chosen.reshape(-1), experts).reshape(tok_count, top_count)
    destination = chosen * capacity + slot_index
    slots = jnp.arange(capacity, dtype=jnp.int32)

    def own_share(array, j):
        return lax.dynamic_slice_in_dim(array, jnp.bitwise_xor(t, j) * share, share, array.ndim - 1)

    normed_shares = [own_share(normed, j) for j in range(tensor_count)]

    def picked_rows(k, j):
        row_index = jnp.bitwise_xor(z, k) * capacity + slots
        matches = jnp.any(destination[None, :, :] == row_index[:, None, None], axis=2)
        return jnp.dot(
            matches.astype(jnp.bfloat16), normed_shares[j], preferred_element_type=jnp.float32
        ).astype(jnp.bfloat16)

    half = max(1, expert_count // 2)
    chunks = [c for c in (range(half), range(half, expert_count)) if len(c)]
    tensor_index = t.astype(jnp.int32).reshape(1)
    weights_of = (w_gate[0], w_up[0], w_down[0])

    arrived = {}
    for chunk in chunks:
        for k in chunk:
            if k:
                arrived[k] = swap(picked_rows(k, 0), "expert", k)

    results = [None] * expert_count
    for number, chunk in enumerate(chunks):
        remote = [k for k in chunk if k]
        if remote:
            mine = jnp.concatenate([arrived[k] for k in remote], axis=0)
            columns = [mine] + [swap(mine, "tensor", j) for j in range(1, tensor_count)]
        if chunk[0] == 0:
            local = [picked_rows(0, j) for j in range(tensor_count)]
        if chunk[0] == 0:
            columns = [
                jnp.concatenate([a, b], axis=0) if remote else a
                for a, b in zip(local, columns if remote else local)
            ]
        rows = jnp.concatenate(columns, axis=1)
        sources = [rows] + [swap(rows, "dp", d) for d in range(1, replica_count)]
        split = number and capacity % 8 == 0
        parts = [[k] for k in chunk] if split else [list(chunk)]
        sums = run_expert(
            sources,
            *weights_of,
            tensor_index,
            tensor_count,
            [capacity * len(part) for part in parts],
        )
        for at, part in enumerate(parts):
            total = sums[at]
            for d in range(1, replica_count):
                total = total + swap(sums[d * len(parts) + at], "dp", d)
            owned = total[:, :share]
            for j in range(1, tensor_count):
                block = total[:, j * share : (j + 1) * share].astype(jnp.bfloat16)
                owned = owned + swap(block, "tensor", j).astype(jnp.float32)
            owned = owned.astype(jnp.bfloat16)
            for i, k in enumerate(part):
                block = owned[i * capacity : (i + 1) * capacity]
                results[k] = swap(block, "expert", k) if k else block

    logits = jnp.dot(normed, w_router, preferred_element_type=jnp.float32)
    selector = (chosen[:, :, None] == jnp.arange(experts, dtype=jnp.int32)[None, None, :]).astype(
        jnp.float32
    )
    picked = jnp.sum(selector * logits[:, None, :], axis=2)
    spread = picked[:, 0] - picked[:, 1]
    gate_values = jnp.stack([jax.nn.sigmoid(spread), jax.nn.sigmoid(-spread)], axis=1)
    row_index = jnp.concatenate(
        [jnp.bitwise_xor(z, k) * capacity + slots for k in range(expert_count)]
    )
    placed = (destination[:, :, None] == row_index[None, None, :]).astype(jnp.float32)
    mixing = jnp.sum(gate_values[:, :, None] * placed, axis=1)
    mixture = jnp.dot(
        mixing,
        jnp.concatenate(results, axis=0).astype(jnp.float32),
        precision=lax.Precision.HIGHEST,
    )
    own_rows = own_share(token_rows, 0)
    outputs = (own_rows + mixture).astype(jnp.bfloat16)
    out_rows = outputs.astype(jnp.float32)
    partial = jnp.stack([jnp.sum(own_rows * out_rows, axis=1), jnp.sum(out_rows * out_rows, axis=1)])
    cross_sum, out_sum = sum_over(partial, "tensor")
    cosine = (
        cross_sum
        / model_width
        * lax.rsqrt((in_squares + EPS_COS) * (out_sum / model_width + EPS_COS))
    )
    local_total = jnp.sum(1.0 - cosine)
    grand_total = sum_over(sum_over(local_total.reshape(1), "dp"), "expert")
    layer_score = grand_total[0] / (tok_count * expert_count * replica_count)
    return (outputs.reshape(1, tok_count, share), layer_score)


def solution(mesh):
    return jax.shard_map(
        shards,
        mesh=mesh,
        in_specs=(
            P("dp", "expert", None),
            P("dp", "expert", None),
            P(),
            P(),
            P("expert", None, ("tensor", "dp")),
            P("expert", None, ("tensor", "dp")),
            P("expert", ("tensor", "dp"), None),
        ),
        out_specs=(P("dp", "expert", "tensor"), P()),
        check_vma=False,
    )
```

profile of v0, /device:TPU:0, one launch (start us, length us, event | category | flops | bytes accessed | tf_op | source)
XLA Modules:
  0.0 148.7 jit_solution(12870550278280051488)
XLA Ops:
  0.7 0.9 copy.31
  1.7 0.2 multiply_reduce_fusion
  2.2 0.7 add_bitcast_fusion
  2.9 1.5 %fusion = f32[128]{0:T(128)S(1)} fusion(bf16[1,128,4096]{2,1,0:T(8,128)(2,1)} %param.7), kind=kLoop, calls=%fused_computation.2 | loop fusion | flops 1572736 | bytes 1049088 | tf_op jit(solution)/shard_map/reduce_sum | solution.py:209
  4.5 0.3 fusion.2
  4.9 0.9 convolution_convert_fusion.5
  5.8 3.1 %collective-permute-start = (bf16[72,1024]{1,0:T(8,128)(2,1)}, bf16[72,1024]{1,0:T(8,128)(2,1)}, u32[]{:S(2)}, u32[]{:S(2)}) collective-permute-start(bf16[72,1024]{1,0:T(8,128)(2,1)} %convolution_convert_fusion.5), channel_id=1, source_target_pairs={{0,8},{8,0},{16,24},{24,16},{1,9},{9,1},{17,25},{25,17},{2,10},{10... | collective-permute-start | bytes 442376 | tf_op jit(solution)/shard_map/ppermute | solution.py:25
  8.8 0.2 convolution_convert_fusion.1
  9.0 2.7 %collective-permute-start.10 = (bf16[72,1024]{1,0:T(8,128)(2,1)S(1)}, bf16[72,1024]{1,0:T(8,128)(2,1)S(1)}, u32[]{:S(2)}, u32[]{:S(2)}) collective-permute-start(bf16[72,1024]{1,0:T(8,128)(2,1)S(1)} %convolution_convert_fusion.1), channel_id=1, source_target_pairs={{0,16},{8,24},{16,0},{24,8},{1,17},{9,25},{17,1},{25,9},{2,18},{10... | collective-permute-start | bytes 442376 | tf_op jit(solution)/shard_map/ppermute | solution.py:25
  11.7 0.2 convolution_convert_fusion
  12.1 0.6 multiply_add_fusion
  12.7 0.8 convolution_convert_fusion.6
  13.5 9.5 %collective-permute-done.10 = bf16[72,1024]{1,0:T(8,128)(2,1)S(1)} collective-permute-done((bf16[72,1024]{1,0:T(8,128)(2,1)S(1)}, bf16[72,1024]{1,0:T(8,128)(2,1)S(1)}, u32[]{:S(2)}, u32[]{:S(2)}) %collective-permute-start.10) | collective-permute-done | bytes 147488 | tf_op jit(solution)/shard_map/ppermute | solution.py:25
  23.1 1.6 %collective-permute-start.12 = (bf16[144,1024]{1,0:T(8,128)(2,1)S(1)}, bf16[144,1024]{1,0:T(8,128)(2,1)S(1)}, u32[]{:S(2)}, u32[]{:S(2)}) collective-permute-start(bf16[144,1024]{1,0:T(8,128)(2,1)S(1)} %constant_dynamic-update-slice_fusion), channel_id=1, source_target_pairs={{0,2},{2,0},{4,6},{6,4},{1,3},{3,1},{5,7},{7,5},{8,10},{10,8},{12,... | collective-permute-start | bytes 884744 | tf_op jit(solution)/shard_map/ppermute | solution.py:25
  24.6 1.5 %collective-permute-start.13 = (bf16[144,1024]{1,0:T(8,128)(2,1)S(1)}, bf16[144,1024]{1,0:T(8,128)(2,1)S(1)}, u32[]{:S(2)}, u32[]{:S(2)}) collective-permute-start(bf16[144,1024]{1,0:T(8,128)(2,1)S(1)} %constant_dynamic-update-slice_fusion), channel_id=1, source_target_pairs={{0,4},{2,6},{4,0},{6,2},{1,5},{3,7},{5,1},{7,3},{8,12},{10,14},{12... | collective-permute-start | bytes 884744 | tf_op jit(solution)/shard_map/ppermute | solution.py:25
  26.1 0.5 collective-permute-start.14
  26.6 0.8 convolution_convert_fusion.2
  27.4 0.4 fusion.49
  27.8 4.7 %collective-permute-done.12 = bf16[144,1024]{1,0:T(8,128)(2,1)S(1)} collective-permute-done((bf16[144,1024]{1,0:T(8,128)(2,1)S(1)}, bf16[144,1024]{1,0:T(8,128)(2,1)S(1)}, u32[]{:S(2)}, u32[]{:S(2)}) %collective-permute-start.12) | collective-permute-done | bytes 294944 | tf_op jit(solution)/shard_map/ppermute | solution.py:25
  32.6 4.4 %collective-permute-done.13 = bf16[144,1024]{1,0:T(8,128)(2,1)S(1)} collective-permute-done((bf16[144,1024]{1,0:T(8,128)(2,1)S(1)}, bf16[144,1024]{1,0:T(8,128)(2,1)S(1)}, u32[]{:S(2)}, u32[]{:S(2)}) %collective-permute-start.13) | collective-permute-done | bytes 294944 | tf_op jit(solution)/shard_map/ppermute | solution.py:25
  37.1 0.8 convolution_convert_fusion.3
  38.0 0.8 convolution_convert_fusion.4
  38.9 1.3 collective-permute-start.1
  40.2 0.8 collective-permute-start.2
  41.0 1.4 collective-permute-start.3
  42.6 3.3 %collective-permute-done.1 = bf16[72,1024]{1,0:T(8,128)(2,1)S(1)} collective-permute-done((bf16[72,1024]{1,0:T(8,128)(2,1)}, bf16[72,1024]{1,0:T(8,128)(2,1)S(1)}, u32[]{:S(2)}, u32[]{:S(2)}) %collective-permute-start.1) | collective-permute-done | bytes 147488 | tf_op jit(solution)/shard_map/ppermute | solution.py:25
  45.9 2.1 %collective-permute-done.2 = bf16[72,1024]{1,0:T(8,128)(2,1)S(1)} collective-permute-done((bf16[72,1024]{1,0:T(8,128)(2,1)}, bf16[72,1024]{1,0:T(8,128)(2,1)S(1)}, u32[]{:S(2)}, u32[]{:S(2)}) %collective-permute-start.2) | collective-permute-done | bytes 147488 | tf_op jit(solution)/shard_map/ppermute | solution.py:25
  48.0 1.5 %collective-permute-done.3 = bf16[72,1024]{1,0:T(8,128)(2,1)S(1)} collective-permute-done((bf16[72,1024]{1,0:T(8,128)(2,1)}, bf16[72,1024]{1,0:T(8,128)(2,1)S(1)}, u32[]{:S(2)}, u32[]{:S(2)}) %collective-permute-start.3) | collective-permute-done | bytes 147488 | tf_op jit(solution)/shard_map/ppermute | solution.py:25
  49.5 1.3 maximum_maximum_fusion.refs_0_
  50.9 19.4 %expert.3 = (f32[72,4096]{1,0:T(8,128)S(1)}, f32[72,4096]{1,0:T(8,128)S(1)}, f32[72,4096]{1,0:T(8,128)S(1)}, f32[72,4096]{1,0:T(8,128)S(1)}) custom-call(s32[1]{0:T(128)} %bitcast.3.t_ref, bf16[144,4096]{1,0:T(8,128)(2,1)S(1)} %pad_maximum_fusion.refs_0_, bf16[144,4096]{1,0:T(8,128)(2,1)S(1)} %collective-permute-done.15.refs_1_, ...), custom_call_target="tpu_custom_call" | custom-call | flops 12683575296 | bytes 51118080 | tf_op jit(solution)/shard_map/expert/pallas_call | solution.py:160
  70.3 0.5 collective-permute-start.16
  70.8 18.8 %expert.2 = (f32[144,4096]{1,0:T(8,128)S(1)}, f32[144,4096]{1,0:T(8,128)S(1)}) custom-call(s32[1]{0:T(128)} %bitcast.3.t_ref, bf16[144,4096]{1,0:T(8,128)(2,1)S(1)} %maximum_maximum_fusion.refs_0_, bf16[144,4096]{1,0:T(8,128)(2,1)S(1)} %collective-permute-done.4.refs_1_, bf16[4096,1792]{1,0:T(8,128)(2,1)} %bitcast.55, bf16[4096,1792]{1,0:T(8,128)(2,1)} %bitcast.57, ...), custom_call_target="tpu_custom_call" | custom-call | flops 12683575296 | bytes 51118080 | tf_op jit(solution)/shard_map/expert/pallas_call | solution.py:160
  89.7 0.5 collective-permute-start.21
  90.4 0.8 collective-permute-start.17
  91.2 1.5 %collective-permute-start.18 = (bf16[72,1024]{1,0:T(8,128)(2,1)S(1)}, bf16[72,1024]{1,0:T(8,128)(2,1)S(1)}, u32[]{:S(2)}, u32[]{:S(2)}) collective-permute-start(bf16[72,1024]{1,0:T(8,128)(2,1)S(1)} %get-tuple-element.31), channel_id=1, source_target_pairs={{0,4},{2,6},{4,0},{6,2},{1,5},{3,7},{5,1},{7,3},{8,12},{10,14},{12... | collective-permute-start | bytes 442376 | tf_op jit(solution)/shard_map/ppermute | solution.py:25
  92.7 1.2 collective-permute-start.19
  93.9 2.0 %collective-permute-done.21 = f32[72,4096]{1,0:T(8,128)S(1)} collective-permute-done((f32[72,4096]{1,0:T(8,128)S(1)}, f32[72,4096]{1,0:T(8,128)S(1)}, u32[]{:S(2)}, u32[]{:S(2)}) %collective-permute-start.21) | collective-permute-done | bytes 1179680 | tf_op jit(solution)/shard_map/ppermute | solution.py:25
  96.1 0.8 collective-permute-start.22
  96.9 1.5 %collective-permute-start.23 = (bf16[72,1024]{1,0:T(8,128)(2,1)S(1)}, bf16[72,1024]{1,0:T(8,128)(2,1)S(1)}, u32[]{:S(2)}, u32[]{:S(2)}) collective-permute-start(bf16[72,1024]{1,0:T(8,128)(2,1)S(1)} %get-tuple-element.34), channel_id=1, source_target_pairs={{0,4},{2,6},{4,0},{6,2},{1,5},{3,7},{5,1},{7,3},{8,12},{10,14},{12... | collective-permute-start | bytes 442376 | tf_op jit(solution)/shard_map/ppermute | solution.py:25
  98.4 0.3 fusion.42
  98.8 1.3 collective-permute-start.24
  100.1 0.8 collective-permute-start.6
  100.9 1.5 %collective-permute-start.7 = (bf16[144,1024]{1,0:T(8,128)(2,1)S(1)}, bf16[144,1024]{1,0:T(8,128)(2,1)S(1)}, u32[]{:S(2)}, u32[]{:S(2)}) collective-permute-start(bf16[144,1024]{1,0:T(8,128)(2,1)S(1)} %get-tuple-element.28), channel_id=1, source_target_pairs={{0,4},{2,6},{4,0},{6,2},{1,5},{3,7},{5,1},{7,3},{8,12},{10,14},{12... | collective-permute-start | bytes 884744 | tf_op jit(solution)/shard_map/ppermute | solution.py:25
  102.4 0.9 collective-permute-done.22
  103.3 1.6 %collective-permute-start.8 = (bf16[144,1024]{1,0:T(8,128)(2,1)S(1)}, bf16[144,1024]{1,0:T(8,128)(2,1)S(1)}, u32[]{:S(2)}, u32[]{:S(2)}) collective-permute-start(bf16[144,1024]{1,0:T(8,128)(2,1)S(1)} %get-tuple-element.27), channel_id=1, source_target_pairs={{0,6},{2,4},{4,2},{6,0},{1,7},{3,5},{5,3},{7,1},{8,14},{10,12},{12... | collective-permute-start | bytes 884744 | tf_op jit(solution)/shard_map/ppermute | solution.py:25
  105.0 1.8 %collective-permute-done.23 = bf16[72,1024]{1,0:T(8,128)(2,1)S(1)} collective-permute-done((bf16[72,1024]{1,0:T(8,128)(2,1)S(1)}, bf16[72,1024]{1,0:T(8,128)(2,1)S(1)}, u32[]{:S(2)}, u32[]{:S(2)}) %collective-permute-start.23) | collective-permute-done | bytes 147488 | tf_op jit(solution)/shard_map/ppermute | solution.py:25
  106.8 5.0 %collective-permute-start.20 = (bf16[72,1024]{1,0:T(8,128)(2,1)S(1)}, bf16[72,1024]{1,0:T(8,128)(2,1)S(1)}, u32[]{:S(2)}, u32[]{:S(2)}) collective-permute-start(bf16[72,1024]{1,0:T(8,128)(2,1)S(1)} %fusion.21), channel_id=1, source_target_pairs={{0,16},{8,24},{16,0},{24,8},{1,17},{9,25},{17,1},{25,9},{2,18},{10... | collective-permute-start | bytes 442376 | tf_op jit(solution)/shard_map/ppermute | solution.py:25
  111.8 1.2 collective-permute-start.25
  113.0 5.9 %collective-permute-done.7 = bf16[144,1024]{1,0:T(8,128)(2,1)S(1)} collective-permute-done((bf16[144,1024]{1,0:T(8,128)(2,1)S(1)}, bf16[144,1024]{1,0:T(8,128)(2,1)S(1)}, u32[]{:S(2)}, u32[]{:S(2)}) %collective-permute-start.7) | collective-permute-done | bytes 294944 | tf_op jit(solution)/shard_map/ppermute | solution.py:25
  119.1 3.8 %collective-permute-start.9 = (bf16[72,1024]{1,0:T(8,128)(2,1)S(1)}, bf16[72,1024]{1,0:T(8,128)(2,1)S(1)}, u32[]{:S(2)}, u32[]{:S(2)}) collective-permute-start(bf16[72,1024]{1,0:T(8,128)(2,1)S(1)} %get-tuple-element.36), channel_id=1, source_target_pairs={{0,8},{8,0},{16,24},{24,16},{1,9},{9,1},{17,25},{25,17},{2,10},{10... | collective-permute-start | bytes 442376 | tf_op jit(solution)/shard_map/ppermute | solution.py:25
  122.9 0.2 convert_element_type.105
  123.1 0.6 copy-done.4
  124.0 2.3 %collective-permute-done.9 = bf16[72,1024]{1,0:T(8,128)(2,1)S(1)} collective-permute-done((bf16[72,1024]{1,0:T(8,128)(2,1)S(1)}, bf16[72,1024]{1,0:T(8,128)(2,1)S(1)}, u32[]{:S(2)}, u32[]{:S(2)}) %collective-permute-start.9) | collective-permute-done | bytes 147488 | tf_op jit(solution)/shard_map/ppermute | solution.py:25
  126.3 1.4 fusion.14
  127.6 1.5 %collective-permute-start.26 = (f32[2,128]{1,0:T(2,128)S(1)}, f32[2,128]{1,0:T(2,128)S(1)}, u32[]{:S(2)}, u32[]{:S(2)}) collective-permute-start(f32[2,128]{1,0:T(2,128)S(1)} %pad_maximum_fusion.2), channel_id=1, source_target_pairs={{0,2},{2,0},{4,6},{6,4},{1,3},{3,1},{5,7},{7,5},{8,10},{10,8},{12,... | collective-permute-start | bytes 3080 | tf_op jit(solution)/shard_map/ppermute | solution.py:25
  129.1 2.1 %collective-permute-done.26 = f32[2,128]{1,0:T(2,128)S(1)} collective-permute-done((f32[2,128]{1,0:T(2,128)S(1)}, f32[2,128]{1,0:T(2,128)S(1)}, u32[]{:S(2)}, u32[]{:S(2)}) %collective-permute-start.26) | collective-permute-done | bytes 1056 | tf_op jit(solution)/shard_map/ppermute | solution.py:25
  131.3 1.3 collective-permute-start.27
  132.6 2.3 %collective-permute-done.27 = f32[2,128]{1,0:T(2,128)S(1)} collective-permute-done((f32[2,128]{1,0:T(2,128)S(1)}, f32[2,128]{1,0:T(2,128)S(1)}, u32[]{:S(2)}, u32[]{:S(2)}) %collective-permute-start.27) | collective-permute-done | bytes 1056 | tf_op jit(solution)/shard_map/ppermute | solution.py:25
  134.9 0.6 subtract_reduce_fusion
  135.6 1.3 collective-permute-done.28
  138.1 3.1 %collective-permute-start.29 = (f32[1]{0:T(128)}, f32[1]{0:T(128)}, u32[]{:S(2)}, u32[]{:S(2)}) collective-permute-start(f32[1]{0:T(128)} %add.195), channel_id=1, source_target_pairs={{0,8},{8,0},{16,24},{24,16},{1,9},{9,1},{17,25},{25,17},{2,10},{10... | collective-permute-start | bytes 20 | tf_op jit(solution)/shard_map/ppermute | solution.py:25
  141.2 0.4 collective-permute-done.29
  142.3 4.4 %collective-permute-start.30 = (f32[1]{0:T(128)}, f32[1]{0:T(128)}, u32[]{:S(2)}, u32[]{:S(2)}) collective-permute-start(f32[1]{0:T(128)} %add.196), channel_id=1, source_target_pairs={{0,16},{8,24},{16,0},{24,8},{1,17},{9,25},{17,1},{25,9},{2,18},{10... | collective-permute-start | bytes 20 | tf_op jit(solution)/shard_map/ppermute | solution.py:25
  146.7 0.2 collective-permute-done.30
  (64 shorter events, 2.2 us)
Async XLA Ops:
  0.6 26.8 %copy-start = (bf16[4096,4]{0,1:T(4,128)(2,1)S(1)}, bf16[4096,4]{0,1:T(4,128)(2,1)}, u32[]{:S(2)}) copy-start(bf16[4096,4]{0,1:T(4,128)(2,1)} %param.10) | copy-start | bytes 98308
  0.6 3.8 %copy-start.2 = (bf16[1,128,4096]{2,1,0:T(8,128)(2,1)S(1)}, bf16[1,128,4096]{2,1,0:T(8,128)(2,1)}, u32[]{:S(2)}) copy-start(bf16[1,128,4096]{2,1,0:T(8,128)(2,1)} %param.7) | copy-start | bytes 3145732
  0.7 3.8 %copy-start.5 = (f32[4096]{0:T(1024)S(1)}, f32[4096]{0:T(1024)}, u32[]{:S(2)}) copy-start(f32[4096]{0:T(1024)} %param.9) | copy-start | bytes 49156
  5.8 33.1 %collective-permute-start = (bf16[72,1024]{1,0:T(8,128)(2,1)}, bf16[72,1024]{1,0:T(8,128)(2,1)}, u32[]{:S(2)}, u32[]{:S(2)}) collective-permute-start(bf16[72,1024]{1,0:T(8,128)(2,1)} %convolution_convert_fusion.5), channel_id=1, source_target_pairs={{0,8},{8,0},{16,24},{24,16},{1,9},{9,1},{17,25},{25,17},{2,10},{10... | collective-permute-start | bytes 442376 | tf_op jit(solution)/shard_map/ppermute | solution.py:25
  9.0 14.0 %collective-permute-start.10 = (bf16[72,1024]{1,0:T(8,128)(2,1)S(1)}, bf16[72,1024]{1,0:T(8,128)(2,1)S(1)}, u32[]{:S(2)}, u32[]{:S(2)}) collective-permute-start(bf16[72,1024]{1,0:T(8,128)(2,1)S(1)} %convolution_convert_fusion.1), channel_id=1, source_target_pairs={{0,16},{8,24},{16,0},{24,8},{1,17},{9,25},{17,1},{25,9},{2,18},{10... | collective-permute-start | bytes 442376 | tf_op jit(solution)/shard_map/ppermute | solution.py:25
  11.8 11.2 %collective-permute-start.11 = (bf16[72,1024]{1,0:T(8,128)(2,1)S(1)}, bf16[72,1024]{1,0:T(8,128)(2,1)S(1)}, u32[]{:S(2)}, u32[]{:S(2)}) collective-permute-start(bf16[72,1024]{1,0:T(8,128)(2,1)S(1)} %convolution_convert_fusion), channel_id=1, source_target_pairs={{0,24},{8,16},{16,8},{24,0},{1,25},{9,17},{17,9},{25,1},{2,26},{10... | collective-permute-start | bytes 442376 | tf_op jit(solution)/shard_map/ppermute | solution.py:25
  23.1 9.5 %collective-permute-start.12 = (bf16[144,1024]{1,0:T(8,128)(2,1)S(1)}, bf16[144,1024]{1,0:T(8,128)(2,1)S(1)}, u32[]{:S(2)}, u32[]{:S(2)}) collective-permute-start(bf16[144,1024]{1,0:T(8,128)(2,1)S(1)} %constant_dynamic-update-slice_fusion), channel_id=1, source_target_pairs={{0,2},{2,0},{4,6},{6,4},{1,3},{3,1},{5,7},{7,5},{8,10},{10,8},{12,... | collective-permute-start | bytes 884744 | tf_op jit(solution)/shard_map/ppermute | solution.py:25
  24.6 12.3 %collective-permute-start.13 = (bf16[144,1024]{1,0:T(8,128)(2,1)S(1)}, bf16[144,1024]{1,0:T(8,128)(2,1)S(1)}, u32[]{:S(2)}, u32[]{:S(2)}) collective-permute-start(bf16[144,1024]{1,0:T(8,128)(2,1)S(1)} %constant_dynamic-update-slice_fusion), channel_id=1, source_target_pairs={{0,4},{2,6},{4,0},{6,2},{1,5},{3,7},{5,1},{7,3},{8,12},{10,14},{12... | collective-permute-start | bytes 884744 | tf_op jit(solution)/shard_map/ppermute | solution.py:25
  26.1 10.8 %collective-permute-start.14 = (bf16[144,1024]{1,0:T(8,128)(2,1)S(1)}, bf16[144,1024]{1,0:T(8,128)(2,1)S(1)}, u32[]{:S(2)}, u32[]{:S(2)}) collective-permute-start(bf16[144,1024]{1,0:T(8,128)(2,1)S(1)} %constant_dynamic-update-slice_fusion), channel_id=1, source_target_pairs={{0,6},{2,4},{4,2},{6,0},{1,7},{3,5},{5,3},{7,1},{8,14},{10,12},{12... | collective-permute-start | bytes 884744 | tf_op jit(solution)/shard_map/ppermute | solution.py:25
  37.0 13.9 %collective-permute-start.15 = (bf16[144,4096]{1,0:T(8,128)(2,1)S(1)}, bf16[144,4096]{1,0:T(8,128)(2,1)S(1)}, u32[]{:S(2)}, u32[]{:S(2)}) collective-permute-start(bf16[144,4096]{1,0:T(8,128)(2,1)S(1)} %pad_maximum_fusion.refs_0_), channel_id=1, source_target_pairs={{0,1},{1,0},{2,3},{3,2},{4,5},{5,4},{6,7},{7,6},{8,9},{9,8},{10,11... | collective-permute-start | bytes 3538952 | tf_op jit(solution)/shard_map/ppermute | solution.py:25
  38.9 7.0 %collective-permute-start.1 = (bf16[72,1024]{1,0:T(8,128)(2,1)}, bf16[72,1024]{1,0:T(8,128)(2,1)S(1)}, u32[]{:S(2)}, u32[]{:S(2)}) collective-permute-start(bf16[72,1024]{1,0:T(8,128)(2,1)} %collective-permute-done), channel_id=1, source_target_pairs={{0,2},{2,0},{4,6},{6,4},{1,3},{3,1},{5,7},{7,5},{8,10},{10,8},{12,... | collective-permute-start | bytes 442376 | tf_op jit(solution)/shard_map/ppermute | solution.py:25
  40.2 7.8 %collective-permute-start.2 = (bf16[72,1024]{1,0:T(8,128)(2,1)}, bf16[72,1024]{1,0:T(8,128)(2,1)S(1)}, u32[]{:S(2)}, u32[]{:S(2)}) collective-permute-start(bf16[72,1024]{1,0:T(8,128)(2,1)} %collective-permute-done), channel_id=1, source_target_pairs={{0,4},{2,6},{4,0},{6,2},{1,5},{3,7},{5,1},{7,3},{8,12},{10,14},{12... | collective-permute-start | bytes 442376 | tf_op jit(solution)/shard_map/ppermute | solution.py:25
  41.0 8.5 %collective-permute-start.3 = (bf16[72,1024]{1,0:T(8,128)(2,1)}, bf16[72,1024]{1,0:T(8,128)(2,1)S(1)}, u32[]{:S(2)}, u32[]{:S(2)}) collective-permute-start(bf16[72,1024]{1,0:T(8,128)(2,1)} %collective-permute-done), channel_id=1, source_target_pairs={{0,6},{2,4},{4,2},{6,0},{1,7},{3,5},{5,3},{7,1},{8,14},{10,12},{12... | collective-permute-start | bytes 442376 | tf_op jit(solution)/shard_map/ppermute | solution.py:25
  50.8 20.0 %collective-permute-start.4 = (bf16[144,4096]{1,0:T(8,128)(2,1)S(1)}, bf16[144,4096]{1,0:T(8,128)(2,1)S(1)}, u32[]{:S(2)}, u32[]{:S(2)}) collective-permute-start(bf16[144,4096]{1,0:T(8,128)(2,1)S(1)} %maximum_maximum_fusion.refs_0_), channel_id=1, source_target_pairs={{0,1},{1,0},{2,3},{3,2},{4,5},{5,4},{6,7},{7,6},{8,9},{9,8},{10,11... | collective-permute-start | bytes 3538952 | tf_op jit(solution)/shard_map/ppermute | solution.py:25
  70.3 19.9 %collective-permute-start.16 = (f32[72,4096]{1,0:T(8,128)S(1)}, f32[72,4096]{1,0:T(8,128)S(1)}, u32[]{:S(2)}, u32[]{:S(2)}) collective-permute-start(f32[72,4096]{1,0:T(8,128)S(1)} %get-tuple-element.11), channel_id=1, source_target_pairs={{0,1},{1,0},{2,3},{3,2},{4,5},{5,4},{6,7},{7,6},{8,9},{9,8},{10,11... | collective-permute-start | bytes 3538952 | tf_op jit(solution)/shard_map/ppermute | solution.py:25
  89.6 7.3 %collective-permute-start.5 = (f32[144,4096]{1,0:T(8,128)S(1)}, f32[144,4096]{1,0:T(8,128)S(1)}, u32[]{:S(2)}, u32[]{:S(2)}) collective-permute-start(f32[144,4096]{1,0:T(8,128)S(1)} %get-tuple-element.9), channel_id=1, source_target_pairs={{0,1},{1,0},{2,3},{3,2},{4,5},{5,4},{6,7},{7,6},{8,9},{9,8},{10,11... | collective-permute-start | bytes 7077896 | tf_op jit(solution)/shard_map/ppermute | solution.py:25
  89.7 6.2 %collective-permute-start.21 = (f32[72,4096]{1,0:T(8,128)S(1)}, f32[72,4096]{1,0:T(8,128)S(1)}, u32[]{:S(2)}, u32[]{:S(2)}) collective-permute-start(f32[72,4096]{1,0:T(8,128)S(1)} %get-tuple-element.13), channel_id=1, source_target_pairs={{0,1},{1,0},{2,3},{3,2},{4,5},{5,4},{6,7},{7,6},{8,9},{9,8},{10,11... | collective-permute-start | bytes 3538952 | tf_op jit(solution)/shard_map/ppermute | solution.py:25
  90.4 8.5 %collective-permute-start.17 = (bf16[72,1024]{1,0:T(8,128)(2,1)S(1)}, bf16[72,1024]{1,0:T(8,128)(2,1)S(1)}, u32[]{:S(2)}, u32[]{:S(2)}) collective-permute-start(bf16[72,1024]{1,0:T(8,128)(2,1)S(1)} %get-tuple-element.29), channel_id=1, source_target_pairs={{0,2},{2,0},{4,6},{6,4},{1,3},{3,1},{5,7},{7,5},{8,10},{10,8},{12,... | collective-permute-start | bytes 442376 | tf_op jit(solution)/shard_map/ppermute | solution.py:25
  91.2 8.9 %collective-permute-start.18 = (bf16[72,1024]{1,0:T(8,128)(2,1)S(1)}, bf16[72,1024]{1,0:T(8,128)(2,1)S(1)}, u32[]{:S(2)}, u32[]{:S(2)}) collective-permute-start(bf16[72,1024]{1,0:T(8,128)(2,1)S(1)} %get-tuple-element.31), channel_id=1, source_target_pairs={{0,4},{2,6},{4,0},{6,2},{1,5},{3,7},{5,1},{7,3},{8,12},{10,14},{12... | collective-permute-start | bytes 442376 | tf_op jit(solution)/shard_map/ppermute | solution.py:25
  92.7 8.1 %collective-permute-start.19 = (bf16[72,1024]{1,0:T(8,128)(2,1)S(1)}, bf16[72,1024]{1,0:T(8,128)(2,1)S(1)}, u32[]{:S(2)}, u32[]{:S(2)}) collective-permute-start(bf16[72,1024]{1,0:T(8,128)(2,1)S(1)} %get-tuple-element.30), channel_id=1, source_target_pairs={{0,6},{2,4},{4,2},{6,0},{1,7},{3,5},{5,3},{7,1},{8,14},{10,12},{12... | collective-permute-start | bytes 442376 | tf_op jit(solution)/shard_map/ppermute | solution.py:25
  96.1 7.2 %collective-permute-start.22 = (bf16[72,1024]{1,0:T(8,128)(2,1)S(1)}, bf16[72,1024]{1,0:T(8,128)(2,1)S(1)}, u32[]{:S(2)}, u32[]{:S(2)}) collective-permute-start(bf16[72,1024]{1,0:T(8,128)(2,1)S(1)} %get-tuple-element.32), channel_id=1, source_target_pairs={{0,2},{2,0},{4,6},{6,4},{1,3},{3,1},{5,7},{7,5},{8,10},{10,8},{12,... | collective-permute-start | bytes 442376 | tf_op jit(solution)/shard_map/ppermute | solution.py:25
  96.9 9.9 %collective-permute-start.23 = (bf16[72,1024]{1,0:T(8,128)(2,1)S(1)}, bf16[72,1024]{1,0:T(8,128)(2,1)S(1)}, u32[]{:S(2)}, u32[]{:S(2)}) collective-permute-start(bf16[72,1024]{1,0:T(8,128)(2,1)S(1)} %get-tuple-element.34), channel_id=1, source_target_pairs={{0,4},{2,6},{4,0},{6,2},{1,5},{3,7},{5,1},{7,3},{8,12},{10,14},{12... | collective-permute-start | bytes 442376 | tf_op jit(solution)/shard_map/ppermute | solution.py:25
  98.8 12.9 %collective-permute-start.24 = (bf16[72,1024]{1,0:T(8,128)(2,1)S(1)}, bf16[72,1024]{1,0:T(8,128)(2,1)S(1)}, u32[]{:S(2)}, u32[]{:S(2)}) collective-permute-start(bf16[72,1024]{1,0:T(8,128)(2,1)S(1)} %get-tuple-element.33), channel_id=1, source_target_pairs={{0,6},{2,4},{4,2},{6,0},{1,7},{3,5},{5,3},{7,1},{8,14},{10,12},{12... | collective-permute-start | bytes 442376 | tf_op jit(solution)/shard_map/ppermute | solution.py:25
  100.1 12.9 %collective-permute-start.6 = (bf16[144,1024]{1,0:T(8,128)(2,1)S(1)}, bf16[144,1024]{1,0:T(8,128)(2,1)S(1)}, u32[]{:S(2)}, u32[]{:S(2)}) collective-permute-start(bf16[144,1024]{1,0:T(8,128)(2,1)S(1)} %get-tuple-element.26), channel_id=1, source_target_pairs={{0,2},{2,0},{4,6},{6,4},{1,3},{3,1},{5,7},{7,5},{8,10},{10,8},{12,... | collective-permute-start | bytes 884744 | tf_op jit(solution)/shard_map/ppermute | solution.py:25
  100.9 18.0 %collective-permute-start.7 = (bf16[144,1024]{1,0:T(8,128)(2,1)S(1)}, bf16[144,1024]{1,0:T(8,128)(2,1)S(1)}, u32[]{:S(2)}, u32[]{:S(2)}) collective-permute-start(bf16[144,1024]{1,0:T(8,128)(2,1)S(1)} %get-tuple-element.28), channel_id=1, source_target_pairs={{0,4},{2,6},{4,0},{6,2},{1,5},{3,7},{5,1},{7,3},{8,12},{10,14},{12... | collective-permute-start | bytes 884744 | tf_op jit(solution)/shard_map/ppermute | solution.py:25
  103.3 15.6 %collective-permute-start.8 = (bf16[144,1024]{1,0:T(8,128)(2,1)S(1)}, bf16[144,1024]{1,0:T(8,128)(2,1)S(1)}, u32[]{:S(2)}, u32[]{:S(2)}) collective-permute-start(bf16[144,1024]{1,0:T(8,128)(2,1)S(1)} %get-tuple-element.27), channel_id=1, source_target_pairs={{0,6},{2,4},{4,2},{6,0},{1,7},{3,5},{5,3},{7,1},{8,14},{10,12},{12... | collective-permute-start | bytes 884744 | tf_op jit(solution)/shard_map/ppermute | solution.py:25
  106.8 17.1 %collective-permute-start.20 = (bf16[72,1024]{1,0:T(8,128)(2,1)S(1)}, bf16[72,1024]{1,0:T(8,128)(2,1)S(1)}, u32[]{:S(2)}, u32[]{:S(2)}) collective-permute-start(bf16[72,1024]{1,0:T(8,128)(2,1)S(1)} %fusion.21), channel_id=1, source_target_pairs={{0,16},{8,24},{16,0},{24,8},{1,17},{9,25},{17,1},{25,9},{2,18},{10... | collective-permute-start | bytes 442376 | tf_op jit(solution)/shard_map/ppermute | solution.py:25
  111.8 12.1 %collective-permute-start.25 = (bf16[72,1024]{1,0:T(8,128)(2,1)S(1)}, bf16[72,1024]{1,0:T(8,128)(2,1)S(1)}, u32[]{:S(2)}, u32[]{:S(2)}) collective-permute-start(bf16[72,1024]{1,0:T(8,128)(2,1)S(1)} %fusion.18), channel_id=1, source_target_pairs={{0,24},{8,16},{16,8},{24,0},{1,25},{9,17},{17,9},{25,1},{2,26},{10... | collective-permute-start | bytes 442376 | tf_op jit(solution)/shard_map/ppermute | solution.py:25
  118.9 4.0 %copy-start.3 = (bf16[1,128,4096]{2,1,0:T(8,128)(2,1)S(1)}, bf16[1,128,4096]{2,1,0:T(8,128)(2,1)}, u32[]{:S(2)}) copy-start(bf16[1,128,4096]{2,1,0:T(8,128)(2,1)} %param.7) | copy-start | bytes 3145732
  119.1 7.2 %collective-permute-start.9 = (bf16[72,1024]{1,0:T(8,128)(2,1)S(1)}, bf16[72,1024]{1,0:T(8,128)(2,1)S(1)}, u32[]{:S(2)}, u32[]{:S(2)}) collective-permute-start(bf16[72,1024]{1,0:T(8,128)(2,1)S(1)} %get-tuple-element.36), channel_id=1, source_target_pairs={{0,8},{8,0},{16,24},{24,16},{1,9},{9,1},{17,25},{25,17},{2,10},{10... | collective-permute-start | bytes 442376 | tf_op jit(solution)/shard_map/ppermute | solution.py:25
  122.9 0.8 copy-start.4
  126.3 21.3 %copy-start.1 = (bf16[4096,4]{0,1:T(4,128)(2,1)S(1)}, bf16[4096,4]{0,1:T(4,128)(2,1)}, u32[]{:S(2)}) copy-start(bf16[4096,4]{0,1:T(4,128)(2,1)} %param.10) | copy-start | bytes 98308
  127.6 3.6 %collective-permute-start.26 = (f32[2,128]{1,0:T(2,128)S(1)}, f32[2,128]{1,0:T(2,128)S(1)}, u32[]{:S(2)}, u32[]{:S(2)}) collective-permute-start(f32[2,128]{1,0:T(2,128)S(1)} %pad_maximum_fusion.2), channel_id=1, source_target_pairs={{0,2},{2,0},{4,6},{6,4},{1,3},{3,1},{5,7},{7,5},{8,10},{10,8},{12,... | collective-permute-start | bytes 3080 | tf_op jit(solution)/shard_map/ppermute | solution.py:25
  131.3 3.6 %collective-permute-start.27 = (f32[2,128]{1,0:T(2,128)S(1)}, f32[2,128]{1,0:T(2,128)S(1)}, u32[]{:S(2)}, u32[]{:S(2)}) collective-permute-start(f32[2,128]{1,0:T(2,128)S(1)} %fusion.41), channel_id=1, source_target_pairs={{0,4},{2,6},{4,0},{6,2},{1,5},{3,7},{5,1},{7,3},{8,12},{10,14},{12... | collective-permute-start | bytes 3080 | tf_op jit(solution)/shard_map/ppermute | solution.py:25
  135.6 1.3 collective-permute-start.28
  138.1 3.6 %collective-permute-start.29 = (f32[1]{0:T(128)}, f32[1]{0:T(128)}, u32[]{:S(2)}, u32[]{:S(2)}) collective-permute-start(f32[1]{0:T(128)} %add.195), channel_id=1, source_target_pairs={{0,8},{8,0},{16,24},{24,16},{1,9},{9,1},{17,25},{25,17},{2,10},{10... | collective-permute-start | bytes 20 | tf_op jit(solution)/shard_map/ppermute | solution.py:25
  142.3 4.6 %collective-permute-start.30 = (f32[1]{0:T(128)}, f32[1]{0:T(128)}, u32[]{:S(2)}, u32[]{:S(2)}) collective-permute-start(f32[1]{0:T(128)} %add.196), channel_id=1, source_target_pairs={{0,16},{8,24},{16,0},{24,8},{1,17},{9,25},{17,1},{25,9},{2,18},{10... | collective-permute-start | bytes 20 | tf_op jit(solution)/shard_map/ppermute | solution.py:25
where the time goes:
time: 149 us
  starting transfers between devices  45.5 us (31%)
  waiting for transfers between devices  44.8 us (30%)
  Pallas kernels  38.1 us (26%)
  other arithmetic  6.93 us (5%)
  matrix products  6.34 us (4%)
  between operations  4.66 us (3%)
  local copies, waits for them, and re-layouts  2.27 us (2%)
    ppermute x31, starting transfers between devices, swap(): return lax.ppermute(value, axis, [(i, i ^ step) for i in range(count)])  45.5 us
    ppermute x31, waiting for transfers between devices, swap(): return lax.ppermute(value, axis, [(i, i ^ step) for i in range(count)])  44.8 us
    pallas_call x2, Pallas kernels, run_expert(): pl.pallas_call(functools.partial(expert_kernel, groups, parts, shares, f_...  38.1 us
    dot_general x7, matrix products, picked_rows(): jnp.dot(matches.astype(jnp.bfloat16), normed_shares[j], preferred_element...  4.6 us
  transfers between devices with their start and end apart: 31, of which 16 were waited for; matrix products, arithmetic and copies ran while one was open for 5% of the time, Pallas kernels for 26%

commit v1 on v0

--- a/solution.py
+++ b/solution.py
@@ -32,36 +32,76 @@
     return size
 
 
-def expert_kernel(groups, parts, shares, f_tiles, n_tiles, t_ref, *refs):
+def hidden_kernel(groups, shares, f_tiles, t_ref, *refs):
     sources = refs[:groups]
-    w_gate, w_up, w_down = refs[groups : groups + 3]
-    results = refs[groups + 3 : groups + 3 + groups * len(parts)]
-    (rows_ref, act_ref, out_ref, gate_buf, up_buf, down_buf) = refs[-10:-4]
-    row_sems, in_sems, down_sems, out_sems = refs[-4:]
+    w_gate, w_up, act_ref, rows_ref, gate_buf, up_buf, row_sems, in_sems = refs[groups:]
     rows = sources[0].shape[0]
     share = sources[0].shape[1] // shares
-    f_tile = gate_buf.shape[2]
-    n_tile = down_buf.shape[2]
-    per = share // n_tile
-
-    def row_copy(d, j):
-        at = pl.multiple_of(jnp.bitwise_xor(t_ref[0], j) * share, share)
-        return pltpu.make_async_copy(
-            sources[d].at[:, pl.ds(j * share, share)],
-            rows_ref.at[pl.ds(d * rows, rows), pl.ds(at, share)],
-            row_sems.at[d, j],
-        )
-
-    def in_copy(weight, buffer, which, f):
-        source = weight
-        if f_tiles > 1:
-            source = weight.at[:, pl.ds(pl.multiple_of(f * f_tile, f_tile), f_tile)]
-        slot = lax.rem(f, gate_buf.shape[0])
-        return pltpu.make_async_copy(source, buffer.at[slot], in_sems.at[which, slot])
+    slots, _, f_tile = gate_buf.shape
+
+    def row_copies():
+        copies = []
+        for d in range(groups):
+            for j in range(shares):
+                at = pl.multiple_of(jnp.bitwise_xor(t_ref[0], j) * share, share)
+                copies.append(
+                    pltpu.make_async_copy(
+                        sources[d].at[:, pl.ds(j * share, share)],
+                        rows_ref.at[pl.ds(d * rows, rows), pl.ds(at, share)],
+                        row_sems.at[d, j],
+                    )
+                )
+        return copies
+
+    def in_copies(f):
+        slot = lax.rem(f, slots)
+        at = pl.ds(pl.multiple_of(f * f_tile, f_tile), f_tile)
+        pairs = ((w_gate, gate_buf), (w_up, up_buf))
+        return [
+            pltpu.make_async_copy(
+                weight.at[:, at] if f_tiles > 1 else weight, buffer.at[slot], in_sems.at[i, slot]
+            )
+            for i, (weight, buffer) in enumerate(pairs)
+        ]
+
+    def start_in(f):
+        for copy in in_copies(f):
+            copy.start()
+
+    for copy in row_copies():
+        copy.start()
+    start_in(0)
+    for copy in row_copies():
+        copy.wait()
+    for f in range(1, min(AHEAD, f_tiles)):
+        start_in(f)
+
+    def step(f, carry):
+        for copy in in_copies(f):
+            copy.wait()
+        pl.when(f + AHEAD < f_tiles)(lambda: start_in(f + AHEAD))
+        slot = lax.rem(f, slots)
+        gate = jnp.dot(rows_ref[...], gate_buf[slot], preferred_element_type=jnp.float32)
+        up = jnp.dot(rows_ref[...], up_buf[slot], preferred_element_type=jnp.float32)
+        act = (gate / (1.0 + jnp.exp(-gate)) * up).astype(jnp.bfloat16)
+        if f_tiles == 1:
+            act_ref[...] = act
+        else:
+            act_ref[:, pl.ds(pl.multiple_of(f * f_tile, f_tile), f_tile)] = act
+        return carry
+
+    lax.fori_loop(0, f_tiles, step, 0)
+
+
+def down_kernel(parts, shares, n_tiles, t_ref, act_ref, w_down, *refs):
+    results = refs[: len(parts)]
+    out_ref, down_buf, down_sems, out_sems = refs[len(parts) :]
+    slots, _, n_tile = down_buf.shape
+    per = n_tiles // shares
 
     def down_copy(n):
-        at = (jnp.bitwise_xor(t_ref[0], n // per) * per + n % per) * n_tile
-        slot = lax.rem(n, down_buf.shape[0])
+        at = (jnp.bitwise_xor(t_ref[0], n // per) * per + lax.rem(n, per)) * n_tile
+        slot = lax.rem(n, slots)
         return pltpu.make_async_copy(
             w_down.at[:, pl.ds(pl.multiple_of(at, n_tile), n_tile)],
             down_buf.at[slot],
@@ -72,8 +112,7 @@
         at = pl.ds(pl.multiple_of(n * n_tile, n_tile), n_tile)
         begin = 0
         copies = []
-        for which in range(groups * len(parts)):
-            size = parts[which % len(parts)]
+        for which, size in enumerate(parts):
             copies.append(
                 pltpu.make_async_copy(
                     out_ref.at[n, pl.ds(begin, size)],
@@ -84,105 +123,85 @@
             begin += size
         return copies
 
-    def start_hidden(f):
-        in_copy(w_gate, gate_buf, 0, f).start()
-        in_copy(w_up, up_buf, 1, f).start()
-
-    def start_down(n):
-        if isinstance(n, int):
-            if n < n_tiles:
-                down_copy(n).start()
-        else:
-            pl.when(n < n_tiles)(lambda: down_copy(n).start())
-
-    for d in range(groups):
-        for j in range(shares):
-            row_copy(d, j).start()
-    start_hidden(0)
-    for d in range(groups):
-        for j in range(shares):
-            row_copy(d, j).wait()
-    for f in range(1, min(AHEAD, f_tiles)):
-        start_hidden(f)
-    for e in range(AHEAD - f_tiles):
-        start_down(2 * e)
-        start_down(2 * e + 1)
-
-    def hidden_step(f, carry):
-        in_copy(w_gate, gate_buf, 0, f).wait()
-        in_copy(w_up, up_buf, 1, f).wait()
-
-        @pl.when(f + AHEAD < f_tiles)
-        def _():
-            start_hidden(f + AHEAD)
-
-        @pl.when(f + AHEAD >= f_tiles)
-        def _():
-            start_down(2 * (f + AHEAD - f_tiles))
-            start_down(2 * (f + AHEAD - f_tiles) + 1)
-
-        slot = lax.rem(f, gate_buf.shape[0])
-        gate = jnp.dot(rows_ref[...], gate_buf[slot], preferred_element_type=jnp.float32)
-        up = jnp.dot(rows_ref[...], up_buf[slot], preferred_element_type=jnp.float32)
-        act = (gate / (1.0 + jnp.exp(-gate)) * up).astype(jnp.bfloat16)
-        if f_tiles == 1:
-            act_ref[...] = act
-        else:
-            act_ref[:, pl.ds(pl.multiple_of(f * f_tile, f_tile), f_tile)] = act
-        return carry
-
-    def down_step(n, carry):
+    for n in range(slots - 1):
+        down_copy(n).start()
+
+    def step(n, carry):
         down_copy(n).wait()
-        start_down(n + 2 * AHEAD)
-        out_ref[n] = jnp.dot(act_ref[...], down_buf[lax.rem(n, down_buf.shape[0])], preferred_element_type=jnp.float32)
+        pl.when(n + slots - 1 < n_tiles)(lambda: down_copy(n + slots - 1).start())
+        out_ref[n] = jnp.dot(
+            act_ref[...], down_buf[lax.rem(n, slots)], preferred_element_type=jnp.float32
+        )
         for copy in out_copies(n):
             copy.start()
         return carry
 
-    lax.fori_loop(0, f_tiles, hidden_step, 0)
-    lax.fori_loop(0, n_tiles, down_step, 0)
+    lax.fori_loop(0, n_tiles, step, 0)
     for n in range(n_tiles):
         for copy in out_copies(n):
             copy.wait()
 
 
-def run_expert(sources, w_gate, w_up, w_down, tensor_index, shares, parts):
+def run_hidden(sources, w_gate, w_up, tensor_index, shares):
     groups = len(sources)
     rows, width = sources[0].shape
     hidden = w_gate.shape[1]
-    share = width // shares
     f_tile = tile_of(hidden, 256)
-    n_tile = tile_of(share, 512)
-    f_tiles, n_tiles = hidden // f_tile, width // n_tile
+    f_tiles = hidden // f_tile
     total = groups * rows
-    in_slots = min(f_tiles, AHEAD + 1)
-    down_slots = min(n_tiles, 2 * AHEAD + 1)
+    slots = min(f_tiles, AHEAD + 1)
     return pl.pallas_call(
-        functools.partial(expert_kernel, groups, parts, shares, f_tiles, n_tiles),
-        out_shape=[jax.ShapeDtypeStruct((size, width), jnp.float32) for size in parts] * groups,
+        functools.partial(hidden_kernel, groups, shares, f_tiles),
+        out_shape=jax.ShapeDtypeStruct((total, hidden), jnp.bfloat16),
         in_specs=[pl.BlockSpec(memory_space=pltpu.SMEM)]
-        + [pl.BlockSpec(memory_space=pl.ANY)] * (groups + 3),
-        out_specs=[pl.BlockSpec(memory_space=pl.ANY)] * (groups * len(parts)),
+        + [pl.BlockSpec(memory_space=pl.ANY)] * (groups + 2),
+        out_specs=pl.BlockSpec(memory_space=pltpu.VMEM),
         scratch_shapes=[
             pltpu.VMEM((total, width), jnp.bfloat16),
-            pltpu.VMEM((total, hidden), jnp.bfloat16),
-            pltpu.VMEM((n_tiles, total, n_tile), jnp.float32),
-            pltpu.VMEM((in_slots, width, f_tile), jnp.bfloat16),
-            pltpu.VMEM((in_slots, width, f_tile), jnp.bfloat16),
-            pltpu.VMEM((down_slots, hidden, n_tile), jnp.bfloat16),
+            pltpu.VMEM((slots, width, f_tile), jnp.bfloat16),
+            pltpu.VMEM((slots, width, f_tile), jnp.bfloat16),
             pltpu.SemaphoreType.DMA((groups, shares)),
-            pltpu.SemaphoreType.DMA((2, in_slots)),
-            pltpu.SemaphoreType.DMA((down_slots,)),
-            pltpu.SemaphoreType.DMA((groups * len(parts), n_tiles)),
+            pltpu.SemaphoreType.DMA((2, slots)),
         ],
-        compiler_params=pltpu.CompilerParams(vmem_limit_bytes=38 << 20),
+        compiler_params=pltpu.CompilerParams(vmem_limit_bytes=44 << 20),
         cost_estimate=pl.CostEstimate(
-            flops=6 * total * width * hidden,
-            bytes_accessed=6 * width * hidden + 6 * total * width,
+            flops=4 * total * width * hidden,
+            bytes_accessed=4 * width * hidden + 2 * total * (width + hidden),
             transcendentals=total * hidden,
         ),
-        name="expert",
-    )(tensor_index, *sources, w_gate, w_up, w_down)
+        name="hidden",
+    )(tensor_index, *sources, w_gate, w_up)
+
+
+def run_down(act, w_down, tensor_index, shares, parts):
+    total, hidden = act.shape
+    width = w_down.shape[1]
+    n_tile = tile_of(width // shares, 512)
+    n_tiles = width // n_tile
+    slots = min(n_tiles, 2 * AHEAD + 1)
+    return pl.pallas_call(
+        functools.partial(down_kernel, parts, shares, n_tiles),
+        out_shape=[jax.ShapeDtypeStruct((size, width), jnp.float32) for size in parts],
+        in_specs=[
+            pl.BlockSpec(memory_space=pltpu.SMEM),
+            pl.BlockSpec(memory_space=pltpu.VMEM),
+            pl.BlockSpec(memory_space=pl.ANY),
+        ],
+        out_specs=[pl.BlockSpec(memory_space=pl.ANY)] * len(parts),
+        scratch_shapes=[
+            pltpu.VMEM((n_tiles, total, n_tile), jnp.float32),
+            pltpu.VMEM((slots, hidden, n_tile), jnp.bfloat16),
+            pltpu.SemaphoreType.DMA((slots,)),
+            pltpu.SemaphoreType.DMA((len(parts), n_tiles)),
+        ],
+        compiler_params=pltpu.CompilerParams(vmem_limit_bytes=44 << 20),
+        cost_estimate=pl.CostEstimate(
+            flops=2 * total * width * hidden,
+            bytes_accessed=2 * width * hidden + 2 * total * hidden + 4 * total * width,
+            transcendentals=0,
+        ),
+        name="down",
+    )(tensor_index, act, w_down)
 
 
 def sum_over(value, axis):
@@ -229,7 +248,6 @@
     half = max(1, expert_count // 2)
     chunks = [c for c in (range(half), range(half, expert_count)) if len(c)]
     tensor_index = t.astype(jnp.int32).reshape(1)
-    weights_of = (w_gate[0], w_up[0], w_down[0])
 
     arrived = {}
     for chunk in chunks:
@@ -254,12 +272,13 @@
         sources = [rows] + [swap(rows, "dp", d) for d in range(1, replica_count)]
         split = number and capacity % 8 == 0
         parts = [[k] for k in chunk] if split else [list(chunk)]
-        sums = run_expert(
-            sources,
-            *weights_of,
+        act = run_hidden(sources, w_gate[0], w_up[0], tensor_index, tensor_count)
+        sums = run_down(
+            act,
+            w_down[0],
             tensor_index,
             tensor_count,
-            [capacity * len(part) for part in parts],
+            [capacity * len(part) for part in parts] * replica_count,
         )
         for at, part in enumerate(parts):
             total = sums[at]

time: 149 us -> 152 us (1.020)
  Pallas kernels: 38.1 us -> 41.1 us
    pallas_call x2 -> x4, Pallas kernels: 38.1 us -> 41.1 us  [the longest x2 24.9 us: run_hidden(): pl.pallas_call(functools.partial(hidden_kernel, groups, shares, f_tiles),...]
  transfers between devices with their start and end apart: 31 -> 31, of which waited for: 16 -> 16; matrix products, arithmetic and copies ran while one was open for 5% -> 5% of each run, Pallas kernels for 26% -> 27%
where the time goes in v1:
time: 152 us
  starting transfers between devices  45.5 us (30%)
  waiting for transfers between devices  44.8 us (29%)
  Pallas kernels  41.1 us (27%)
  other arithmetic  6.93 us (5%)
  matrix products  6.34 us (4%)
  between operations  4.68 us (3%)
  local copies, waits for them, and re-layouts  2.27 us (1%)
    ppermute x31, starting transfers between devices, swap(): return lax.ppermute(value, axis, [(i, i ^ step) for i in range(count)])  45.5 us
    ppermute x31, waiting for transfers between devices, swap(): return lax.ppermute(value, axis, [(i, i ^ step) for i in range(count)])  44.8 us
    pallas_call x2, Pallas kernels, run_hidden(): pl.pallas_call(functools.partial(hidden_kernel, groups, shares, f_tiles),...  24.9 us
    pallas_call x2, Pallas kernels, run_down(): pl.pallas_call(functools.partial(down_kernel, parts, shares, n_tiles), ou...  16.2 us
    dot_general x7, matrix products, picked_rows(): jnp.dot(matches.astype(jnp.bfloat16), normed_shares[j], preferred_element...  4.6 us
  transfers between devices with their start and end apart: 31, of which 16 were waited for; matrix products, arithmetic and copies ran while one was open for 5% of the time, Pallas kernels for 27%

profile of v1, /device:TPU:0, one launch (start us, length us, event | category | flops | bytes accessed | tf_op | source)
XLA Modules:
  0.0 151.6 jit_solution(12020998627451031163)
XLA Ops:
  0.7 0.9 copy.31
  1.7 0.2 multiply_reduce_fusion
  2.2 0.7 add_bitcast_fusion
  2.9 1.5 %fusion = f32[128]{0:T(128)S(1)} fusion(bf16[1,128,4096]{2,1,0:T(8,128)(2,1)} %param.7), kind=kLoop, calls=%fused_computation.2 | loop fusion | flops 1572736 | bytes 1049088 | tf_op jit(solution)/shard_map/reduce_sum | solution.py:228
  4.5 0.3 fusion.2
  4.9 0.9 convolution_convert_fusion.5
  5.8 3.1 %collective-permute-start = (bf16[72,1024]{1,0:T(8,128)(2,1)}, bf16[72,1024]{1,0:T(8,128)(2,1)}, u32[]{:S(2)}, u32[]{:S(2)}) collective-permute-start(bf16[72,1024]{1,0:T(8,128)(2,1)} %convolution_convert_fusion.5), channel_id=1, source_target_pairs={{0,8},{8,0},{16,24},{24,16},{1,9},{9,1},{17,25},{25,17},{2,10},{10... | collective-permute-start | bytes 442376 | tf_op jit(solution)/shard_map/ppermute | solution.py:25
  9.0 2.7 %collective-permute-start.10 = (bf16[72,1024]{1,0:T(8,128)(2,1)S(1)}, bf16[72,1024]{1,0:T(8,128)(2,1)S(1)}, u32[]{:S(2)}, u32[]{:S(2)}) collective-permute-start(bf16[72,1024]{1,0:T(8,128)(2,1)S(1)} %convolution_convert_fusion.1), channel_id=1, source_target_pairs={{0,16},{8,24},{16,0},{24,8},{1,17},{9,25},{17,1},{25,9},{2,18},{10... | collective-permute-start | bytes 442376 | tf_op jit(solution)/shard_map/ppermute | solution.py:25
  12.1 0.6 multiply_add_fusion
  12.7 0.8 convolution_convert_fusion.6
  13.5 9.5 %collective-permute-done.10 = bf16[72,1024]{1,0:T(8,128)(2,1)S(1)} collective-permute-done((bf16[72,1024]{1,0:T(8,128)(2,1)S(1)}, bf16[72,1024]{1,0:T(8,128)(2,1)S(1)}, u32[]{:S(2)}, u32[]{:S(2)}) %collective-permute-start.10) | collective-permute-done | bytes 147488 | tf_op jit(solution)/shard_map/ppermute | solution.py:25
  23.1 1.6 %collective-permute-start.12 = (bf16[144,1024]{1,0:T(8,128)(2,1)S(1)}, bf16[144,1024]{1,0:T(8,128)(2,1)S(1)}, u32[]{:S(2)}, u32[]{:S(2)}) collective-permute-start(bf16[144,1024]{1,0:T(8,128)(2,1)S(1)} %constant_dynamic-update-slice_fusion), channel_id=1, source_target_pairs={{0,2},{2,0},{4,6},{6,4},{1,3},{3,1},{5,7},{7,5},{8,10},{10,8},{12,... | collective-permute-start | bytes 884744 | tf_op jit(solution)/shard_map/ppermute | solution.py:25
  24.6 1.5 %collective-permute-start.13 = (bf16[144,1024]{1,0:T(8,128)(2,1)S(1)}, bf16[144,1024]{1,0:T(8,128)(2,1)S(1)}, u32[]{:S(2)}, u32[]{:S(2)}) collective-permute-start(bf16[144,1024]{1,0:T(8,128)(2,1)S(1)} %constant_dynamic-update-slice_fusion), channel_id=1, source_target_pairs={{0,4},{2,6},{4,0},{6,2},{1,5},{3,7},{5,1},{7,3},{8,12},{10,14},{12... | collective-permute-start | bytes 884744 | tf_op jit(solution)/shard_map/ppermute | solution.py:25
  26.1 0.5 collective-permute-start.14
  26.6 0.8 convolution_convert_fusion.2
  27.4 0.4 fusion.49
  27.8 4.7 %collective-permute-done.12 = bf16[144,1024]{1,0:T(8,128)(2,1)S(1)} collective-permute-done((bf16[144,1024]{1,0:T(8,128)(2,1)S(1)}, bf16[144,1024]{1,0:T(8,128)(2,1)S(1)}, u32[]{:S(2)}, u32[]{:S(2)}) %collective-permute-start.12) | collective-permute-done | bytes 294944 | tf_op jit(solution)/shard_map/ppermute | solution.py:25
  32.6 4.4 %collective-permute-done.13 = bf16[144,1024]{1,0:T(8,128)(2,1)S(1)} collective-permute-done((bf16[144,1024]{1,0:T(8,128)(2,1)S(1)}, bf16[144,1024]{1,0:T(8,128)(2,1)S(1)}, u32[]{:S(2)}, u32[]{:S(2)}) %collective-permute-start.13) | collective-permute-done | bytes 294944 | tf_op jit(solution)/shard_map/ppermute | solution.py:25
  37.1 0.8 convolution_convert_fusion.3
  38.0 0.8 convolution_convert_fusion.4
  38.9 1.3 collective-permute-start.1
  40.2 0.8 collective-permute-start.2
  41.0 1.4 collective-permute-start.3
  42.6 3.3 %collective-permute-done.1 = bf16[72,1024]{1,0:T(8,128)(2,1)S(1)} collective-permute-done((bf16[72,1024]{1,0:T(8,128)(2,1)}, bf16[72,1024]{1,0:T(8,128)(2,1)S(1)}, u32[]{:S(2)}, u32[]{:S(2)}) %collective-permute-start.1) | collective-permute-done | bytes 147488 | tf_op jit(solution)/shard_map/ppermute | solution.py:25
  45.9 2.1 %collective-permute-done.2 = bf16[72,1024]{1,0:T(8,128)(2,1)S(1)} collective-permute-done((bf16[72,1024]{1,0:T(8,128)(2,1)}, bf16[72,1024]{1,0:T(8,128)(2,1)S(1)}, u32[]{:S(2)}, u32[]{:S(2)}) %collective-permute-start.2) | collective-permute-done | bytes 147488 | tf_op jit(solution)/shard_map/ppermute | solution.py:25
  48.0 1.5 %collective-permute-done.3 = bf16[72,1024]{1,0:T(8,128)(2,1)S(1)} collective-permute-done((bf16[72,1024]{1,0:T(8,128)(2,1)}, bf16[72,1024]{1,0:T(8,128)(2,1)S(1)}, u32[]{:S(2)}, u32[]{:S(2)}) %collective-permute-start.3) | collective-permute-done | bytes 147488 | tf_op jit(solution)/shard_map/ppermute | solution.py:25
  49.5 1.3 maximum_maximum_fusion.refs_0_
  50.9 12.5 %hidden.3.act_ref = bf16[288,1792]{1,0:T(8,128)(2,1)S(1)} custom-call(s32[1]{0:T(128)} %bitcast.3.t_ref, bf16[144,4096]{1,0:T(8,128)(2,1)S(1)} %pad_maximum_fusion.refs_0_, bf16[144,4096]{1,0:T(8,128)(2,1)S(1)} %collective-permute-done.15.refs_1_, bf16[4096,1792]{1,0:T(8,128)(2,1)} %bitcast.47, bf16[4096,1792]{1,0:T(8,128)(2,1)} %bitcast.49), custom_call_target="tpu_custom_call" | custom-call | flops 8455716864 | bytes 32751616 | tf_op jit(solution)/shard_map/hidden/pallas_call | solution.py:153
  63.4 8.4 %down.3 = (f32[72,4096]{1,0:T(8,128)S(1)}, f32[72,4096]{1,0:T(8,128)S(1)}, f32[72,4096]{1,0:T(8,128)S(1)}, f32[72,4096]{1,0:T(8,128)S(1)}) custom-call(s32[1]{0:T(128)} %bitcast.3.t_ref, bf16[288,1792]{1,0:T(8,128)(2,1)S(1)} %hidden.3.act_ref, bf16[1792,4096]{1,0:T(8,128)(2,1)} %bitcast.51), custom_call_target="tpu_custom_call" | custom-call | flops 4227858432 | bytes 20430848 | tf_op jit(solution)/shard_map/down/pallas_call | solution.py:182
  71.7 0.6 collective-permute-start.16
  72.3 12.5 %hidden.2.act_ref = bf16[288,1792]{1,0:T(8,128)(2,1)S(1)} custom-call(s32[1]{0:T(128)} %bitcast.3.t_ref, bf16[144,4096]{1,0:T(8,128)(2,1)S(1)} %maximum_maximum_fusion.refs_0_, bf16[144,4096]{1,0:T(8,128)(2,1)S(1)} %collective-permute-done.4.refs_1_, bf16[4096,1792]{1,0:T(8,128)(2,1)} %bitcast.48, bf16[4096,1792]{1,0:T(8,128)(2,1)} %bitcast.50), custom_call_target="tpu_custom_call" | custom-call | flops 8455716864 | bytes 32751616 | tf_op jit(solution)/shard_map/hidden/pallas_call | solution.py:153
  84.8 7.8 %down.2 = (f32[144,4096]{1,0:T(8,128)S(1)}, f32[144,4096]{1,0:T(8,128)S(1)}) custom-call(s32[1]{0:T(128)} %bitcast.3.t_ref, bf16[288,1792]{1,0:T(8,128)(2,1)S(1)} %hidden.2.act_ref, bf16[1792,4096]{1,0:T(8,128)(2,1)} %bitcast.52), custom_call_target="tpu_custom_call" | custom-call | flops 4227858432 | bytes 20430848 | tf_op jit(solution)/shard_map/down/pallas_call | solution.py:182
  92.6 0.5 collective-permute-start.21
  93.3 0.8 collective-permute-start.17
  94.2 1.5 %collective-permute-start.18 = (bf16[72,1024]{1,0:T(8,128)(2,1)S(1)}, bf16[72,1024]{1,0:T(8,128)(2,1)S(1)}, u32[]{:S(2)}, u32[]{:S(2)}) collective-permute-start(bf16[72,1024]{1,0:T(8,128)(2,1)S(1)} %get-tuple-element.31), channel_id=1, source_target_pairs={{0,4},{2,6},{4,0},{6,2},{1,5},{3,7},{5,1},{7,3},{8,12},{10,14},{12... | collective-permute-start | bytes 442376 | tf_op jit(solution)/shard_map/ppermute | solution.py:25
  95.7 1.2 collective-permute-start.19
  96.9 2.0 %collective-permute-done.21 = f32[72,4096]{1,0:T(8,128)S(1)} collective-permute-done((f32[72,4096]{1,0:T(8,128)S(1)}, f32[72,4096]{1,0:T(8,128)S(1)}, u32[]{:S(2)}, u32[]{:S(2)}) %collective-permute-start.21) | collective-permute-done | bytes 1179680 | tf_op jit(solution)/shard_map/ppermute | solution.py:25
  99.0 0.8 collective-permute-start.22
  99.9 1.5 %collective-permute-start.23 = (bf16[72,1024]{1,0:T(8,128)(2,1)S(1)}, bf16[72,1024]{1,0:T(8,128)(2,1)S(1)}, u32[]{:S(2)}, u32[]{:S(2)}) collective-permute-start(bf16[72,1024]{1,0:T(8,128)(2,1)S(1)} %get-tuple-element.34), channel_id=1, source_target_pairs={{0,4},{2,6},{4,0},{6,2},{1,5},{3,7},{5,1},{7,3},{8,12},{10,14},{12... | collective-permute-start | bytes 442376 | tf_op jit(solution)/shard_map/ppermute | solution.py:25
  101.4 0.3 fusion.42
  101.8 1.3 collective-permute-start.24
  103.0 0.8 collective-permute-start.6
  103.8 1.5 %collective-permute-start.7 = (bf16[144,1024]{1,0:T(8,128)(2,1)S(1)}, bf16[144,1024]{1,0:T(8,128)(2,1)S(1)}, u32[]{:S(2)}, u32[]{:S(2)}) collective-permute-start(bf16[144,1024]{1,0:T(8,128)(2,1)S(1)} %get-tuple-element.28), channel_id=1, source_target_pairs={{0,4},{2,6},{4,0},{6,2},{1,5},{3,7},{5,1},{7,3},{8,12},{10,14},{12... | collective-permute-start | bytes 884744 | tf_op jit(solution)/shard_map/ppermute | solution.py:25
  105.3 0.9 collective-permute-done.22
  106.2 1.6 %collective-permute-start.8 = (bf16[144,1024]{1,0:T(8,128)(2,1)S(1)}, bf16[144,1024]{1,0:T(8,128)(2,1)S(1)}, u32[]{:S(2)}, u32[]{:S(2)}) collective-permute-start(bf16[144,1024]{1,0:T(8,128)(2,1)S(1)} %get-tuple-element.27), channel_id=1, source_target_pairs={{0,6},{2,4},{4,2},{6,0},{1,7},{3,5},{5,3},{7,1},{8,14},{10,12},{12... | collective-permute-start | bytes 884744 | tf_op jit(solution)/shard_map/ppermute | solution.py:25
  107.9 1.8 %collective-permute-done.23 = bf16[72,1024]{1,0:T(8,128)(2,1)S(1)} collective-permute-done((bf16[72,1024]{1,0:T(8,128)(2,1)S(1)}, bf16[72,1024]{1,0:T(8,128)(2,1)S(1)}, u32[]{:S(2)}, u32[]{:S(2)}) %collective-permute-start.23) | collective-permute-done | bytes 147488 | tf_op jit(solution)/shard_map/ppermute | solution.py:25
  109.7 4.9 %collective-permute-start.20 = (bf16[72,1024]{1,0:T(8,128)(2,1)S(1)}, bf16[72,1024]{1,0:T(8,128)(2,1)S(1)}, u32[]{:S(2)}, u32[]{:S(2)}) collective-permute-start(bf16[72,1024]{1,0:T(8,128)(2,1)S(1)} %fusion.21), channel_id=1, source_target_pairs={{0,16},{8,24},{16,0},{24,8},{1,17},{9,25},{17,1},{25,9},{2,18},{10... | collective-permute-start | bytes 442376 | tf_op jit(solution)/shard_map/ppermute | solution.py:25
  114.7 1.3 collective-permute-start.25
  116.0 5.8 %collective-permute-done.7 = bf16[144,1024]{1,0:T(8,128)(2,1)S(1)} collective-permute-done((bf16[144,1024]{1,0:T(8,128)(2,1)S(1)}, bf16[144,1024]{1,0:T(8,128)(2,1)S(1)}, u32[]{:S(2)}, u32[]{:S(2)}) %collective-permute-start.7) | collective-permute-done | bytes 294944 | tf_op jit(solution)/shard_map/ppermute | solution.py:25
  122.0 3.8 %collective-permute-start.9 = (bf16[72,1024]{1,0:T(8,128)(2,1)S(1)}, bf16[72,1024]{1,0:T(8,128)(2,1)S(1)}, u32[]{:S(2)}, u32[]{:S(2)}) collective-permute-start(bf16[72,1024]{1,0:T(8,128)(2,1)S(1)} %get-tuple-element.36), channel_id=1, source_target_pairs={{0,8},{8,0},{16,24},{24,16},{1,9},{9,1},{17,25},{25,17},{2,10},{10... | collective-permute-start | bytes 442376 | tf_op jit(solution)/shard_map/ppermute | solution.py:25
  125.9 0.2 convert_element_type.105
  126.1 0.6 copy-done.4
  126.9 2.3 %collective-permute-done.9 = bf16[72,1024]{1,0:T(8,128)(2,1)S(1)} collective-permute-done((bf16[72,1024]{1,0:T(8,128)(2,1)S(1)}, bf16[72,1024]{1,0:T(8,128)(2,1)S(1)}, u32[]{:S(2)}, u32[]{:S(2)}) %collective-permute-start.9) | collective-permute-done | bytes 147488 | tf_op jit(solution)/shard_map/ppermute | solution.py:25
  129.2 1.4 fusion.14
  130.6 1.5 collective-permute-start.26
  132.1 2.1 %collective-permute-done.26 = f32[2,128]{1,0:T(2,128)S(1)} collective-permute-done((f32[2,128]{1,0:T(2,128)S(1)}, f32[2,128]{1,0:T(2,128)S(1)}, u32[]{:S(2)}, u32[]{:S(2)}) %collective-permute-start.26) | collective-permute-done | bytes 1056 | tf_op jit(solution)/shard_map/ppermute | solution.py:25
  134.2 1.3 collective-permute-start.27
  135.5 2.3 %collective-permute-done.27 = f32[2,128]{1,0:T(2,128)S(1)} collective-permute-done((f32[2,128]{1,0:T(2,128)S(1)}, f32[2,128]{1,0:T(2,128)S(1)}, u32[]{:S(2)}, u32[]{:S(2)}) %collective-permute-start.27) | collective-permute-done | bytes 1056 | tf_op jit(solution)/shard_map/ppermute | solution.py:25
  137.9 0.6 subtract_reduce_fusion
  138.5 1.3 collective-permute-done.28
  141.0 3.1 %collective-permute-start.29 = (f32[1]{0:T(128)}, f32[1]{0:T(128)}, u32[]{:S(2)}, u32[]{:S(2)}) collective-permute-start(f32[1]{0:T(128)} %add.195), channel_id=1, source_target_pairs={{0,8},{8,0},{16,24},{24,16},{1,9},{9,1},{17,25},{25,17},{2,10},{10... | collective-permute-start | bytes 20 | tf_op jit(solution)/shard_map/ppermute | solution.py:25
  144.2 0.4 collective-permute-done.29
  145.3 4.3 %collective-permute-start.30 = (f32[1]{0:T(128)}, f32[1]{0:T(128)}, u32[]{:S(2)}, u32[]{:S(2)}) collective-permute-start(f32[1]{0:T(128)} %add.196), channel_id=1, source_target_pairs={{0,16},{8,24},{16,0},{24,8},{1,17},{9,25},{17,1},{25,9},{2,18},{10... | collective-permute-start | bytes 20 | tf_op jit(solution)/shard_map/ppermute | solution.py:25
  149.6 0.2 collective-permute-done.30
  (66 shorter events, 2.6 us)
Async XLA Ops:
  0.6 26.8 %copy-start = (bf16[4096,4]{0,1:T(4,128)(2,1)S(1)}, bf16[4096,4]{0,1:T(4,128)(2,1)}, u32[]{:S(2)}) copy-start(bf16[4096,4]{0,1:T(4,128)(2,1)} %param.10) | copy-start | bytes 98308
  0.6 3.8 %copy-start.2 = (bf16[1,128,4096]{2,1,0:T(8,128)(2,1)S(1)}, bf16[1,128,4096]{2,1,0:T(8,128)(2,1)}, u32[]{:S(2)}) copy-start(bf16[1,128,4096]{2,1,0:T(8,128)(2,1)} %param.7) | copy-start | bytes 3145732
  0.7 3.8 %copy-start.5 = (f32[4096]{0:T(1024)S(1)}, f32[4096]{0:T(1024)}, u32[]{:S(2)}) copy-start(f32[4096]{0:T(1024)} %param.9) | copy-start | bytes 49156
  5.8 33.1 %collective-permute-start = (bf16[72,1024]{1,0:T(8,128)(2,1)}, bf16[72,1024]{1,0:T(8,128)(2,1)}, u32[]{:S(2)}, u32[]{:S(2)}) collective-permute-start(bf16[72,1024]{1,0:T(8,128)(2,1)} %convolution_convert_fusion.5), channel_id=1, source_target_pairs={{0,8},{8,0},{16,24},{24,16},{1,9},{9,1},{17,25},{25,17},{2,10},{10... | collective-permute-start | bytes 442376 | tf_op jit(solution)/shard_map/ppermute | solution.py:25
  9.0 14.0 %collective-permute-start.10 = (bf16[72,1024]{1,0:T(8,128)(2,1)S(1)}, bf16[72,1024]{1,0:T(8,128)(2,1)S(1)}, u32[]{:S(2)}, u32[]{:S(2)}) collective-permute-start(bf16[72,1024]{1,0:T(8,128)(2,1)S(1)} %convolution_convert_fusion.1), channel_id=1, source_target_pairs={{0,16},{8,24},{16,0},{24,8},{1,17},{9,25},{17,1},{25,9},{2,18},{10... | collective-permute-start | bytes 442376 | tf_op jit(solution)/shard_map/ppermute | solution.py:25
  11.8 11.2 %collective-permute-start.11 = (bf16[72,1024]{1,0:T(8,128)(2,1)S(1)}, bf16[72,1024]{1,0:T(8,128)(2,1)S(1)}, u32[]{:S(2)}, u32[]{:S(2)}) collective-permute-start(bf16[72,1024]{1,0:T(8,128)(2,1)S(1)} %convolution_convert_fusion), channel_id=1, source_target_pairs={{0,24},{8,16},{16,8},{24,0},{1,25},{9,17},{17,9},{25,1},{2,26},{10... | collective-permute-start | bytes 442376 | tf_op jit(solution)/shard_map/ppermute | solution.py:25
  23.1 9.5 %collective-permute-start.12 = (bf16[144,1024]{1,0:T(8,128)(2,1)S(1)}, bf16[144,1024]{1,0:T(8,128)(2,1)S(1)}, u32[]{:S(2)}, u32[]{:S(2)}) collective-permute-start(bf16[144,1024]{1,0:T(8,128)(2,1)S(1)} %constant_dynamic-update-slice_fusion), channel_id=1, source_target_pairs={{0,2},{2,0},{4,6},{6,4},{1,3},{3,1},{5,7},{7,5},{8,10},{10,8},{12,... | collective-permute-start | bytes 884744 | tf_op jit(solution)/shard_map/ppermute | solution.py:25
  24.6 12.3 %collective-permute-start.13 = (bf16[144,1024]{1,0:T(8,128)(2,1)S(1)}, bf16[144,1024]{1,0:T(8,128)(2,1)S(1)}, u32[]{:S(2)}, u32[]{:S(2)}) collective-permute-start(bf16[144,1024]{1,0:T(8,128)(2,1)S(1)} %constant_dynamic-update-slice_fusion), channel_id=1, source_target_pairs={{0,4},{2,6},{4,0},{6,2},{1,5},{3,7},{5,1},{7,3},{8,12},{10,14},{12... | collective-permute-start | bytes 884744 | tf_op jit(solution)/shard_map/ppermute | solution.py:25
  26.1 10.8 %collective-permute-start.14 = (bf16[144,1024]{1,0:T(8,128)(2,1)S(1)}, bf16[144,1024]{1,0:T(8,128)(2,1)S(1)}, u32[]{:S(2)}, u32[]{:S(2)}) collective-permute-start(bf16[144,1024]{1,0:T(8,128)(2,1)S(1)} %constant_dynamic-update-slice_fusion), channel_id=1, source_target_pairs={{0,6},{2,4},{4,2},{6,0},{1,7},{3,5},{5,3},{7,1},{8,14},{10,12},{12... | collective-permute-start | bytes 884744 | tf_op jit(solution)/shard_map/ppermute | solution.py:25
  37.0 13.9 %collective-permute-start.15 = (bf16[144,4096]{1,0:T(8,128)(2,1)S(1)}, bf16[144,4096]{1,0:T(8,128)(2,1)S(1)}, u32[]{:S(2)}, u32[]{:S(2)}) collective-permute-start(bf16[144,4096]{1,0:T(8,128)(2,1)S(1)} %pad_maximum_fusion.refs_0_), channel_id=1, source_target_pairs={{0,1},{1,0},{2,3},{3,2},{4,5},{5,4},{6,7},{7,6},{8,9},{9,8},{10,11... | collective-permute-start | bytes 3538952 | tf_op jit(solution)/shard_map/ppermute | solution.py:25
  38.9 7.0 %collective-permute-start.1 = (bf16[72,1024]{1,0:T(8,128)(2,1)}, bf16[72,1024]{1,0:T(8,128)(2,1)S(1)}, u32[]{:S(2)}, u32[]{:S(2)}) collective-permute-start(bf16[72,1024]{1,0:T(8,128)(2,1)} %collective-permute-done), channel_id=1, source_target_pairs={{0,2},{2,0},{4,6},{6,4},{1,3},{3,1},{5,7},{7,5},{8,10},{10,8},{12,... | collective-permute-start | bytes 442376 | tf_op jit(solution)/shard_map/ppermute | solution.py:25
  40.2 7.8 %collective-permute-start.2 = (bf16[72,1024]{1,0:T(8,128)(2,1)}, bf16[72,1024]{1,0:T(8,128)(2,1)S(1)}, u32[]{:S(2)}, u32[]{:S(2)}) collective-permute-start(bf16[72,1024]{1,0:T(8,128)(2,1)} %collective-permute-done), channel_id=1, source_target_pairs={{0,4},{2,6},{4,0},{6,2},{1,5},{3,7},{5,1},{7,3},{8,12},{10,14},{12... | collective-permute-start | bytes 442376 | tf_op jit(solution)/shard_map/ppermute | solution.py:25
  41.0 8.5 %collective-permute-start.3 = (bf16[72,1024]{1,0:T(8,128)(2,1)}, bf16[72,1024]{1,0:T(8,128)(2,1)S(1)}, u32[]{:S(2)}, u32[]{:S(2)}) collective-permute-start(bf16[72,1024]{1,0:T(8,128)(2,1)} %collective-permute-done), channel_id=1, source_target_pairs={{0,6},{2,4},{4,2},{6,0},{1,7},{3,5},{5,3},{7,1},{8,14},{10,12},{12... | collective-permute-start | bytes 442376 | tf_op jit(solution)/shard_map/ppermute | solution.py:25
  50.8 21.5 %collective-permute-start.4 = (bf16[144,4096]{1,0:T(8,128)(2,1)S(1)}, bf16[144,4096]{1,0:T(8,128)(2,1)S(1)}, u32[]{:S(2)}, u32[]{:S(2)}) collective-permute-start(bf16[144,4096]{1,0:T(8,128)(2,1)S(1)} %maximum_maximum_fusion.refs_0_), channel_id=1, source_target_pairs={{0,1},{1,0},{2,3},{3,2},{4,5},{5,4},{6,7},{7,6},{8,9},{9,8},{10,11... | collective-permute-start | bytes 3538952 | tf_op jit(solution)/shard_map/ppermute | solution.py:25
  71.7 21.4 %collective-permute-start.16 = (f32[72,4096]{1,0:T(8,128)S(1)}, f32[72,4096]{1,0:T(8,128)S(1)}, u32[]{:S(2)}, u32[]{:S(2)}) collective-permute-start(f32[72,4096]{1,0:T(8,128)S(1)} %get-tuple-element.11), channel_id=1, source_target_pairs={{0,1},{1,0},{2,3},{3,2},{4,5},{5,4},{6,7},{7,6},{8,9},{9,8},{10,11... | collective-permute-start | bytes 3538952 | tf_op jit(solution)/shard_map/ppermute | solution.py:25
  92.5 7.3 %collective-permute-start.5 = (f32[144,4096]{1,0:T(8,128)S(1)}, f32[144,4096]{1,0:T(8,128)S(1)}, u32[]{:S(2)}, u32[]{:S(2)}) collective-permute-start(f32[144,4096]{1,0:T(8,128)S(1)} %get-tuple-element.9), channel_id=1, source_target_pairs={{0,1},{1,0},{2,3},{3,2},{4,5},{5,4},{6,7},{7,6},{8,9},{9,8},{10,11... | collective-permute-start | bytes 7077896 | tf_op jit(solution)/shard_map/ppermute | solution.py:25
  92.6 6.2 %collective-permute-start.21 = (f32[72,4096]{1,0:T(8,128)S(1)}, f32[72,4096]{1,0:T(8,128)S(1)}, u32[]{:S(2)}, u32[]{:S(2)}) collective-permute-start(f32[72,4096]{1,0:T(8,128)S(1)} %get-tuple-element.13), channel_id=1, source_target_pairs={{0,1},{1,0},{2,3},{3,2},{4,5},{5,4},{6,7},{7,6},{8,9},{9,8},{10,11... | collective-permute-start | bytes 3538952 | tf_op jit(solution)/shard_map/ppermute | solution.py:25
  93.3 8.4 %collective-permute-start.17 = (bf16[72,1024]{1,0:T(8,128)(2,1)S(1)}, bf16[72,1024]{1,0:T(8,128)(2,1)S(1)}, u32[]{:S(2)}, u32[]{:S(2)}) collective-permute-start(bf16[72,1024]{1,0:T(8,128)(2,1)S(1)} %get-tuple-element.29), channel_id=1, source_target_pairs={{0,2},{2,0},{4,6},{6,4},{1,3},{3,1},{5,7},{7,5},{8,10},{10,8},{12,... | collective-permute-start | bytes 442376 | tf_op jit(solution)/shard_map/ppermute | solution.py:25
  94.2 8.9 %collective-permute-start.18 = (bf16[72,1024]{1,0:T(8,128)(2,1)S(1)}, bf16[72,1024]{1,0:T(8,128)(2,1)S(1)}, u32[]{:S(2)}, u32[]{:S(2)}) collective-permute-start(bf16[72,1024]{1,0:T(8,128)(2,1)S(1)} %get-tuple-element.31), channel_id=1, source_target_pairs={{0,4},{2,6},{4,0},{6,2},{1,5},{3,7},{5,1},{7,3},{8,12},{10,14},{12... | collective-permute-start | bytes 442376 | tf_op jit(solution)/shard_map/ppermute | solution.py:25
  95.7 8.1 %collective-permute-start.19 = (bf16[72,1024]{1,0:T(8,128)(2,1)S(1)}, bf16[72,1024]{1,0:T(8,128)(2,1)S(1)}, u32[]{:S(2)}, u32[]{:S(2)}) collective-permute-start(bf16[72,1024]{1,0:T(8,128)(2,1)S(1)} %get-tuple-element.30), channel_id=1, source_target_pairs={{0,6},{2,4},{4,2},{6,0},{1,7},{3,5},{5,3},{7,1},{8,14},{10,12},{12... | collective-permute-start | bytes 442376 | tf_op jit(solution)/shard_map/ppermute | solution.py:25
  99.0 7.2 %collective-permute-start.22 = (bf16[72,1024]{1,0:T(8,128)(2,1)S(1)}, bf16[72,1024]{1,0:T(8,128)(2,1)S(1)}, u32[]{:S(2)}, u32[]{:S(2)}) collective-permute-start(bf16[72,1024]{1,0:T(8,128)(2,1)S(1)} %get-tuple-element.32), channel_id=1, source_target_pairs={{0,2},{2,0},{4,6},{6,4},{1,3},{3,1},{5,7},{7,5},{8,10},{10,8},{12,... | collective-permute-start | bytes 442376 | tf_op jit(solution)/shard_map/ppermute | solution.py:25
  99.9 9.9 %collective-permute-start.23 = (bf16[72,1024]{1,0:T(8,128)(2,1)S(1)}, bf16[72,1024]{1,0:T(8,128)(2,1)S(1)}, u32[]{:S(2)}, u32[]{:S(2)}) collective-permute-start(bf16[72,1024]{1,0:T(8,128)(2,1)S(1)} %get-tuple-element.34), channel_id=1, source_target_pairs={{0,4},{2,6},{4,0},{6,2},{1,5},{3,7},{5,1},{7,3},{8,12},{10,14},{12... | collective-permute-start | bytes 442376 | tf_op jit(solution)/shard_map/ppermute | solution.py:25
  101.8 12.9 %collective-permute-start.24 = (bf16[72,1024]{1,0:T(8,128)(2,1)S(1)}, bf16[72,1024]{1,0:T(8,128)(2,1)S(1)}, u32[]{:S(2)}, u32[]{:S(2)}) collective-permute-start(bf16[72,1024]{1,0:T(8,128)(2,1)S(1)} %get-tuple-element.33), channel_id=1, source_target_pairs={{0,6},{2,4},{4,2},{6,0},{1,7},{3,5},{5,3},{7,1},{8,14},{10,12},{12... | collective-permute-start | bytes 442376 | tf_op jit(solution)/shard_map/ppermute | solution.py:25
  103.0 13.0 %collective-permute-start.6 = (bf16[144,1024]{1,0:T(8,128)(2,1)S(1)}, bf16[144,1024]{1,0:T(8,128)(2,1)S(1)}, u32[]{:S(2)}, u32[]{:S(2)}) collective-permute-start(bf16[144,1024]{1,0:T(8,128)(2,1)S(1)} %get-tuple-element.26), channel_id=1, source_target_pairs={{0,2},{2,0},{4,6},{6,4},{1,3},{3,1},{5,7},{7,5},{8,10},{10,8},{12,... | collective-permute-start | bytes 884744 | tf_op jit(solution)/shard_map/ppermute | solution.py:25
  103.8 18.0 %collective-permute-start.7 = (bf16[144,1024]{1,0:T(8,128)(2,1)S(1)}, bf16[144,1024]{1,0:T(8,128)(2,1)S(1)}, u32[]{:S(2)}, u32[]{:S(2)}) collective-permute-start(bf16[144,1024]{1,0:T(8,128)(2,1)S(1)} %get-tuple-element.28), channel_id=1, source_target_pairs={{0,4},{2,6},{4,0},{6,2},{1,5},{3,7},{5,1},{7,3},{8,12},{10,14},{12... | collective-permute-start | bytes 884744 | tf_op jit(solution)/shard_map/ppermute | solution.py:25
  106.2 15.6 %collective-permute-start.8 = (bf16[144,1024]{1,0:T(8,128)(2,1)S(1)}, bf16[144,1024]{1,0:T(8,128)(2,1)S(1)}, u32[]{:S(2)}, u32[]{:S(2)}) collective-permute-start(bf16[144,1024]{1,0:T(8,128)(2,1)S(1)} %get-tuple-element.27), channel_id=1, source_target_pairs={{0,6},{2,4},{4,2},{6,0},{1,7},{3,5},{5,3},{7,1},{8,14},{10,12},{12... | collective-permute-start | bytes 884744 | tf_op jit(solution)/shard_map/ppermute | solution.py:25
  109.7 17.2 %collective-permute-start.20 = (bf16[72,1024]{1,0:T(8,128)(2,1)S(1)}, bf16[72,1024]{1,0:T(8,128)(2,1)S(1)}, u32[]{:S(2)}, u32[]{:S(2)}) collective-permute-start(bf16[72,1024]{1,0:T(8,128)(2,1)S(1)} %fusion.21), channel_id=1, source_target_pairs={{0,16},{8,24},{16,0},{24,8},{1,17},{9,25},{17,1},{25,9},{2,18},{10... | collective-permute-start | bytes 442376 | tf_op jit(solution)/shard_map/ppermute | solution.py:25
  114.7 12.2 %collective-permute-start.25 = (bf16[72,1024]{1,0:T(8,128)(2,1)S(1)}, bf16[72,1024]{1,0:T(8,128)(2,1)S(1)}, u32[]{:S(2)}, u32[]{:S(2)}) collective-permute-start(bf16[72,1024]{1,0:T(8,128)(2,1)S(1)} %fusion.18), channel_id=1, source_target_pairs={{0,24},{8,16},{16,8},{24,0},{1,25},{9,17},{17,9},{25,1},{2,26},{10... | collective-permute-start | bytes 442376 | tf_op jit(solution)/shard_map/ppermute | solution.py:25
  121.8 4.0 %copy-start.3 = (bf16[1,128,4096]{2,1,0:T(8,128)(2,1)S(1)}, bf16[1,128,4096]{2,1,0:T(8,128)(2,1)}, u32[]{:S(2)}) copy-start(bf16[1,128,4096]{2,1,0:T(8,128)(2,1)} %param.7) | copy-start | bytes 3145732
  122.0 7.2 %collective-permute-start.9 = (bf16[72,1024]{1,0:T(8,128)(2,1)S(1)}, bf16[72,1024]{1,0:T(8,128)(2,1)S(1)}, u32[]{:S(2)}, u32[]{:S(2)}) collective-permute-start(bf16[72,1024]{1,0:T(8,128)(2,1)S(1)} %get-tuple-element.36), channel_id=1, source_target_pairs={{0,8},{8,0},{16,24},{24,16},{1,9},{9,1},{17,25},{25,17},{2,10},{10... | collective-permute-start | bytes 442376 | tf_op jit(solution)/shard_map/ppermute | solution.py:25
  125.9 0.8 copy-start.4
  129.2 21.2 %copy-start.1 = (bf16[4096,4]{0,1:T(4,128)(2,1)S(1)}, bf16[4096,4]{0,1:T(4,128)(2,1)}, u32[]{:S(2)}) copy-start(bf16[4096,4]{0,1:T(4,128)(2,1)} %param.10) | copy-start | bytes 98308
  130.6 3.6 %collective-permute-start.26 = (f32[2,128]{1,0:T(2,128)S(1)}, f32[2,128]{1,0:T(2,128)S(1)}, u32[]{:S(2)}, u32[]{:S(2)}) collective-permute-start(f32[2,128]{1,0:T(2,128)S(1)} %pad_maximum_fusion.2), channel_id=1, source_target_pairs={{0,2},{2,0},{4,6},{6,4},{1,3},{3,1},{5,7},{7,5},{8,10},{10,8},{12,... | collective-permute-start | bytes 3080 | tf_op jit(solution)/shard_map/ppermute | solution.py:25
  134.2 3.6 %collective-permute-start.27 = (f32[2,128]{1,0:T(2,128)S(1)}, f32[2,128]{1,0:T(2,128)S(1)}, u32[]{:S(2)}, u32[]{:S(2)}) collective-permute-start(f32[2,128]{1,0:T(2,128)S(1)} %fusion.41), channel_id=1, source_target_pairs={{0,4},{2,6},{4,0},{6,2},{1,5},{3,7},{5,1},{7,3},{8,12},{10,14},{12... | collective-permute-start | bytes 3080 | tf_op jit(solution)/shard_map/ppermute | solution.py:25
  138.5 1.3 collective-permute-start.28
  141.0 3.6 %collective-permute-start.29 = (f32[1]{0:T(128)}, f32[1]{0:T(128)}, u32[]{:S(2)}, u32[]{:S(2)}) collective-permute-start(f32[1]{0:T(128)} %add.195), channel_id=1, source_target_pairs={{0,8},{8,0},{16,24},{24,16},{1,9},{9,1},{17,25},{25,17},{2,10},{10... | collective-permute-start | bytes 20 | tf_op jit(solution)/shard_map/ppermute | solution.py:25
  145.3 4.6 %collective-permute-start.30 = (f32[1]{0:T(128)}, f32[1]{0:T(128)}, u32[]{:S(2)}, u32[]{:S(2)}) collective-permute-start(f32[1]{0:T(128)} %add.196), channel_id=1, source_target_pairs={{0,16},{8,24},{16,0},{24,8},{1,17},{9,25},{17,1},{25,9},{2,18},{10... | collective-permute-start | bytes 20 | tf_op jit(solution)/shard_map/ppermute | solution.py:25
